TPU v7x, 256 devices: a 8x8x2 block of a 8x8x16 slice. The times are simulated.
256 devices in a mesh: groups: 2 (over z), expert: 64 (over x, y), replica: 2 (over core).
Axes of the slice: x: 8, y: 8, z: 2, core: 2. Of those that a mesh axis runs over, the one named last changes fastest.
The devices are a block of a 8x8x16 slice.
Arguments:
- queries: bfloat16 [1024, 8192], P(('groups', 'expert', 'replica')), parts along dimension 0, may hold values from -250 to 250
- token_keys: bfloat16 [1024, 512], P(('groups', 'expert', 'replica')), parts along dimension 0, may hold values from -6 to 6
- token_values: bfloat16 [1024, 512], P(('groups', 'expert', 'replica')), parts along dimension 0, may hold values from -6 to 6
- stored_keys: bfloat16 [1024, 256, 512], P(('groups', 'expert', 'replica')), parts along dimension 0, may hold values from -7 to 7
- stored_values: bfloat16 [1024, 256, 512], P(('groups', 'expert', 'replica')), parts along dimension 0, may hold values from -6 to 6
- kv_len: int32 [1024], P(('groups', 'expert', 'replica')), parts along dimension 0, may hold values from 2 to 256, as said below
- residual: bfloat16 [1024, 4096], P(('groups', 'expert', 'replica')), parts along dimension 0, may hold values from -6 to 6
- out_weight: bfloat16 [8192, 4096], P(('expert', 'replica')), may hold values from -0.1875 to 0.1875
- norm_gain: bfloat16 [4096], replicated, may hold values from 0.25 to 1.75
- expert_ids: int32 [1024, 8], P(('groups', 'expert')), parts along dimension 0, may hold values from 0 to 63, all different within a row; in each aligned block of 8 rows (0 to 7, 8 to 15, ...) at most 2 rows name the same one
- route_weight: float32 [1024, 8], P(('groups', 'expert')), parts along dimension 0, may hold values from 0.05 to 1
- w_gate: bfloat16 [64, 4096, 768], P('expert', None, 'replica'), may hold values from -0.09375 to 0.09375
- w_up: bfloat16 [64, 4096, 768], P('expert', None, 'replica'), may hold values from -0.09375 to 0.09375
- w_down: bfloat16 [64, 768, 4096], P('expert', 'replica'), may hold values from -0.4375 to 0.4375
Outputs:
- updated: bfloat16 [1024, 4096], P(('groups', 'expert', 'replica')), parts along dimension 0
There are 2 independent parts, one for each index of `groups`. A program takes and returns all parts, laid end to end along the dimension named above; an argument that names none is the same for every part. Nothing has to cross between parts.
Inputs may be any that keep to these rules, and one draw needn't show every extreme that they name: `kv_len`: at least 2; some sequence uses all 256 positions. `expert_ids`: each token names 8 different experts; in each aligned block of 8 tokens no expert is named by more than 2 tokens, and some block reaches it.
All inputs are finite; a program needn't handle non-finite values.
Results may differ from a plain program's by a relative error of at most 0.01.
Values may be sent and summed in bfloat16 or wider, within the bound.
A program may use at most 64 MiB of HBM per device.

v0:
```python
import math

import jax
import jax.numpy as jnp
from jax import lax
from jax.sharding import PartitionSpec as P

HEAD_WIDTH = 128


def shifted(block, axis, distance):
    devices = range(lax.axis_size(axis))
    route = [(i - distance, i) for i in devices if i - distance in devices]
    return lax.ppermute(block, axis, route)


def sent_to_all(x, axis):
    copies = jnp.broadcast_to(x, (lax.axis_size(axis), *x.shape))
    return lax.all_to_all(copies, axis, split_axis=0, concat_axis=0, tiled=True)


def laid_out(parts, dim):
    shape = list(parts.shape[1:])
    shape[dim] *= parts.shape[0]
    return jnp.moveaxis(parts, 0, dim).reshape(shape)


def gathered_copies(x, axis, dim):
    parts = sent_to_all(x, axis)
    return laid_out(parts, dim)


def split_up(x, dim, size):
    shape = x.shape
    parts = x.reshape(*shape[:dim], size, shape[dim] // size, *shape[dim + 1 :])
    return jnp.moveaxis(parts, dim, 0)


def sent_and_summed(x, axis, dim):
    size = lax.axis_size(axis)
    parts = lax.all_to_all(split_up(x, dim, size), axis, 0, 0, tiled=True)
    return jnp.sum(parts.astype(jnp.float32), axis=0)


def attend_local(queries, token_keys, token_values, stored_keys, stored_values, kv_len):
    seq_count = queries.shape[0]
    cache_len = stored_keys.shape[1]
    kv_count = token_keys.shape[1] // HEAD_WIDTH
    query_group_width = queries.shape[1] // HEAD_WIDTH // kv_count
    query_head_rows = queries.reshape(seq_count, kv_count, query_group_width, HEAD_WIDTH)
    keys_from_cache = stored_keys.reshape(seq_count, cache_len, kv_count, HEAD_WIDTH)
    values_from_cache = stored_values.reshape(seq_count, cache_len, kv_count, HEAD_WIDTH)
    keys_latest = token_keys.reshape(seq_count, kv_count, HEAD_WIDTH)
    values_latest = token_values.astype(jnp.float32).reshape(seq_count, kv_count, HEAD_WIDTH)
    inv_root = 1.0 / math.sqrt(HEAD_WIDTH)
    cached_scores = (
        jnp.einsum(
            "bgqd,bpgd->bgqp", query_head_rows, keys_from_cache, preferred_element_type=jnp.float32
        )
        * inv_root
    )
    positions = lax.broadcasted_iota(jnp.int32, (seq_count, cache_len), 1)
    visible = positions < kv_len[:, None]
    cached_scores = jnp.where(visible[:, None, None, :], cached_scores, -jnp.inf)
    fresh_score = (
        jnp.einsum(
            "bgqd,bgd->bgq", query_head_rows, keys_latest, preferred_element_type=jnp.float32
        )
        * inv_root
    )
    highest = jnp.maximum(jnp.max(cached_scores, axis=-1), fresh_score)
    cached_exp = jnp.exp(cached_scores - highest[..., None])
    fresh_exp = jnp.exp(fresh_score - highest)
    totals = jnp.sum(cached_exp, axis=-1) + fresh_exp
    cached_prob = (cached_exp / totals[..., None]).astype(jnp.bfloat16)
    fresh_prob = lax.optimization_barrier((fresh_exp / totals).astype(jnp.bfloat16)).astype(
        jnp.float32
    )
    mixed = jnp.einsum(
        "bgqp,bpgd->bgqd", cached_prob, values_from_cache, preferred_element_type=jnp.float32
    )
    mixed = mixed + fresh_prob[..., None] * values_latest[:, :, None, :]
    return mixed.reshape(seq_count, -1).astype(jnp.bfloat16)


def on_device(
    queries,
    token_keys,
    token_values,
    stored_keys,
    stored_values,
    kv_len,
    residual,
    out_weight,
    norm_gain,
    expert_ids,
    route_weight,
    w_gate,
    w_up,
    w_down,
):
    attended = attend_local(queries, token_keys, token_values, stored_keys, stored_values, kv_len)
    column_groups = 8
    device_count = lax.axis_size(("expert", "replica"))
    seq_count, feature_total = attended.shape
    row_count, model_width = out_weight.shape
    feature_groups = device_count // column_groups
    feature_block = feature_total // feature_groups
    col_width = model_width // column_groups
    device_rank = lax.axis_index(("expert", "replica"))
    block_place = device_rank % column_groups
    slot_ids = jnp.arange(column_groups, dtype=jnp.int32)
    own_piece = lax.dynamic_slice_in_dim(out_weight, block_place * col_width, col_width, 1)
    empty_block = jnp.zeros((column_groups, row_count, col_width), out_weight.dtype)
    stacked = jnp.where((slot_ids == block_place)[:, None, None], own_piece[None], empty_block)
    for offset in range(1 - column_groups, column_groups):
        if offset != 0:
            target_place = (device_rank + offset) % column_groups
            sent_piece = lax.dynamic_slice_in_dim(
                out_weight, target_place * col_width, col_width, 1
            )
            arrived_piece = shifted(sent_piece, ("expert", "replica"), offset)
            stacked = jnp.where(
                (slot_ids == block_place - offset)[:, None, None], arrived_piece[None], stacked
            )
    weight_block = stacked.reshape(column_groups * row_count, col_width)
    repeated = jnp.repeat(
        attended.reshape(seq_count, feature_groups, feature_block), column_groups, axis=1
    )
    all_tokens = lax.all_to_all(
        repeated, ("expert", "replica"), split_axis=1, concat_axis=0, tiled=True
    )
    all_tokens = all_tokens.reshape(-1, feature_block)
    partial_cols = jnp.dot(all_tokens, weight_block, preferred_element_type=jnp.float32)
    partial_cols = partial_cols.reshape(-1, 1, col_width)
    came_back = lax.all_to_all(
        partial_cols.astype(jnp.bfloat16),
        ("expert", "replica"),
        split_axis=0,
        concat_axis=1,
        tiled=True,
    ).astype(partial_cols.dtype)
    projected = jnp.sum(
        came_back.reshape(seq_count, feature_groups, column_groups, col_width), axis=1
    ).reshape(seq_count, model_width)
    hidden_state = residual.astype(jnp.float32) + projected
    mean_square = jnp.mean(hidden_state * hidden_state, axis=-1, keepdims=True)
    normed = (hidden_state * lax.rsqrt(mean_square + 1e-06) * norm_gain.astype(jnp.float32)).astype(
        jnp.bfloat16
    )
    pair_tokens = gathered_copies(normed, "replica", 0)
    token_count, topk_count = expert_ids.shape
    expert_count = lax.axis_size("expert")
    capacity = max(2, -(-(token_count * topk_count) // expert_count))
    flat_ids = expert_ids.reshape(-1)
    row_total = flat_ids.shape[0]
    same_expert = flat_ids[:, None] == flat_ids[None, :]
    row_iota = lax.broadcasted_iota(jnp.int32, (row_total, row_total), 0)
    col_iota = lax.broadcasted_iota(jnp.int32, (row_total, row_total), 1)
    slot_ranks = jnp.sum(jnp.where(same_expert & (col_iota < row_iota), 1, 0), axis=1).astype(
        jnp.int32
    )
    slot_of = (flat_ids * capacity + slot_ranks).reshape(token_count, topk_count)
    slot_total = expert_count * capacity
    slot_iota = jnp.arange(slot_total, dtype=jnp.int32)
    slot_hits = slot_of[None, :, :] == slot_iota[:, None, None]
    pick_table = jnp.sum(slot_hits.astype(jnp.float32), axis=2).astype(jnp.bfloat16)
    outgoing = jnp.dot(pick_table, pair_tokens, preferred_element_type=jnp.float32).astype(
        jnp.bfloat16
    )
    outgoing = outgoing.reshape(expert_count, capacity, -1)
    mixing = route_weight / jnp.sum(route_weight, axis=1, keepdims=True)
    combine_rows = jnp.sum(jnp.where(slot_hits, mixing[None, :, :], 0.0), axis=2).T
    incoming = lax.all_to_all(outgoing, "expert", split_axis=0, concat_axis=0, tiled=True)
    model_width = incoming.shape[-1]
    lead_shape = incoming.shape[:2]
    slot_rows = incoming.reshape(-1, model_width)
    gate_act = jnp.dot(slot_rows, w_gate[0], preferred_element_type=jnp.float32)
    up_act = jnp.dot(slot_rows, w_up[0], preferred_element_type=jnp.float32)
    hidden_act = (jax.nn.silu(gate_act) * up_act).astype(jnp.bfloat16)
    partial_value = jnp.dot(hidden_act, w_down[0], preferred_element_type=jnp.float32).reshape(
        lead_shape + (model_width,)
    )
    arrived = lax.all_to_all(
        partial_value.astype(jnp.bfloat16), "expert", split_axis=0, concat_axis=0, tiled=True
    ).astype(partial_value.dtype)
    returned = arrived
    returned = returned.reshape(slot_total, -1)
    pair_moe = jnp.dot(combine_rows, returned, preferred_element_type=jnp.float32)
    moe_out = sent_and_summed(pair_moe.astype(jnp.bfloat16), "replica", 0)
    return (hidden_state + moe_out).astype(jnp.bfloat16)


def solution(mesh):
    in_specs = (
        P(("groups", "expert", "replica"), None),
        P(("groups", "expert", "replica"), None),
        P(("groups", "expert", "replica"), None),
        P(("groups", "expert", "replica"), None, None),
        P(("groups", "expert", "replica"), None, None),
        P(("groups", "expert", "replica")),
        P(("groups", "expert", "replica"), None),
        P(("expert", "replica"), None),
        P(),
        P(("groups", "expert"), None),
        P(("groups", "expert"), None),
        P("expert", None, "replica"),
        P("expert", None, "replica"),
        P("expert", "replica", None),
    )
    out_specs = P(("groups", "expert", "replica"), None)
    return jax.shard_map(
        on_device, mesh=mesh, in_specs=in_specs, out_specs=out_specs, check_vma=False
    )
```

profile of v0, /device:TPU:513, one launch (start us, length us, event | category | flops | bytes accessed | tf_op | source)
XLA Modules:
  0.0 251.0 jit_solution(15461882330532982091)
XLA Ops:
  0.0 0.9 iota_compare_fusion.2
  0.9 0.8 reshape.609
  1.7 0.7 reshape.602
  2.4 0.8 copy.40
  3.3 1.7 fusion.25
  5.3 1.5 fusion.13
  7.0 0.9 broadcast_in_dim.239
  7.9 28.1 %all-to-all-start = ((bf16[4,128,512]{2,0,1:T(4,128)(2,1)}), bf16[4,128,512]{2,0,1:T(4,128)(2,1)}, u32[]{:S(2)}, u32[]{:S(2)}) async-start(bf16[4,128,512]{2,0,1:T(4,128)(2,1)} %bitcast.68), calls=%async_computation | async-start | bytes 1048576 | tf_op jit(solution)/shard_map/all_to_all | solution.py:130
  36.3 2.2 constant_dynamic-slice_fusion.14
  38.5 7.6 %collective-permute-start = (bf16[64,512]{1,0:T(8,128)(2,1)}, bf16[64,512]{1,0:T(8,128)(2,1)S(1)}, u32[]{:S(2)}, u32[]{:S(2)}) collective-permute-start(bf16[64,512]{1,0:T(8,128)(2,1)} %get-tuple-element.7), channel_id=1, source_target_pairs={{0,7},{1,8},{2,9},{3,10},{4,11},{5,12},{6,13},{7,14},{8,15},{9,16}... | collective-permute-start | bytes 196616 | tf_op jit(solution)/shard_map/ppermute | solution.py:14
  46.1 1.3 collective-permute-start.12
  47.4 1.3 collective-permute-start.11
  48.7 1.3 collective-permute-start.10
  50.0 1.3 collective-permute-start.9
  51.5 1.3 collective-permute-start.8
  52.8 9.0 %collective-permute-done.12 = bf16[64,512]{1,0:T(8,128)(2,1)} collective-permute-done((bf16[64,512]{1,0:T(8,128)(2,1)}, bf16[64,512]{1,0:T(8,128)(2,1)}, u32[]{:S(2)}, u32[]{:S(2)}) %collective-permute-start.12) | collective-permute-done | bytes 65568 | tf_op jit(solution)/shard_map/ppermute | solution.py:14
  61.8 1.9 collective-permute-start.7
  63.7 3.7 %collective-permute-start.6 = (bf16[64,512]{1,0:T(8,128)(2,1)}, bf16[64,512]{1,0:T(8,128)(2,1)S(1)}, u32[]{:S(2)}, u32[]{:S(2)}) collective-permute-start(bf16[64,512]{1,0:T(8,128)(2,1)} %get-tuple-element.14), channel_id=1, source_target_pairs={{0,1},{1,2},{2,3},{3,4},{4,5},{5,6},{6,7},{7,8},{8,9},{9,10},{10,1... | collective-permute-start | bytes 196616 | tf_op jit(solution)/shard_map/ppermute | solution.py:14
  67.4 1.3 collective-permute-start.5
  68.8 2.7 %collective-permute-start.4 = (bf16[64,512]{1,0:T(8,128)(2,1)}, bf16[64,512]{1,0:T(8,128)(2,1)S(1)}, u32[]{:S(2)}, u32[]{:S(2)}) collective-permute-start(bf16[64,512]{1,0:T(8,128)(2,1)} %get-tuple-element.16), channel_id=1, source_target_pairs={{0,3},{1,4},{2,5},{3,6},{4,7},{5,8},{6,9},{7,10},{8,11},{9,12},{10... | collective-permute-start | bytes 196616 | tf_op jit(solution)/shard_map/ppermute | solution.py:14
  71.5 2.4 collective-permute-start.3
  74.0 8.8 %collective-permute-start.2 = (bf16[64,512]{1,0:T(8,128)(2,1)S(1)}, bf16[64,512]{1,0:T(8,128)(2,1)S(1)}, u32[]{:S(2)}, u32[]{:S(2)}) collective-permute-start(bf16[64,512]{1,0:T(8,128)(2,1)S(1)} %get-tuple-element.18), channel_id=1, source_target_pairs={{0,5},{1,6},{2,7},{3,8},{4,9},{5,10},{6,11},{7,12},{8,13},{9,14},{... | collective-permute-start | bytes 196616 | tf_op jit(solution)/shard_map/ppermute | solution.py:14
  82.8 4.9 %collective-permute-start.1 = (bf16[64,512]{1,0:T(8,128)(2,1)S(1)}, bf16[64,512]{1,0:T(8,128)(2,1)S(1)}, u32[]{:S(2)}, u32[]{:S(2)}) collective-permute-start(bf16[64,512]{1,0:T(8,128)(2,1)S(1)} %get-tuple-element.19), channel_id=1, source_target_pairs={{0,6},{1,7},{2,8},{3,9},{4,10},{5,11},{6,12},{7,13},{8,14},{9,15},... | collective-permute-start | bytes 196616 | tf_op jit(solution)/shard_map/ppermute | solution.py:14
  87.7 1.3 collective-permute-start.13
  89.1 8.8 %collective-permute-done.13 = bf16[64,512]{1,0:T(8,128)(2,1)S(1)} collective-permute-done((bf16[64,512]{1,0:T(8,128)(2,1)S(1)}, bf16[64,512]{1,0:T(8,128)(2,1)S(1)}, u32[]{:S(2)}, u32[]{:S(2)}) %collective-permute-start.13) | collective-permute-done | bytes 65568 | tf_op jit(solution)/shard_map/ppermute | solution.py:14
  97.8 2.5 select_select_fusion
  100.3 2.0 reshape.595
  102.3 2.4 fusion.5
  105.2 2.7 %reduce = bf16[512,512]{1,0:T(8,128)(2,1)} reduce(bf16[512,1,512]{2,0,1:T(8,128)(2,1)} %fusion.5, bf16[]{:T(256)} %broadcast.557), dimensions={1}, to_apply=%copy.32.reduce_sub_computation | reduce | bytes 1048578 | tf_op jit(solution)/shard_map/convert_element_type | solution.py:137
  108.0 2.2 reshape.610
  110.1 16.1 %all-to-all-start.1 = ((bf16[128,2,1024]{2,1,0:T(2,128)(2,1)}), bf16[128,2,1024]{2,1,0:T(2,128)(2,1)}, u32[]{:S(2)}, u32[]{:S(2)}) async-start(bf16[128,2,1024]{2,1,0:T(2,128)(2,1)} %reshape.610), calls=%async_computation.1 | async-start | bytes 1048576 | tf_op jit(solution)/shard_map/all_to_all | solution.py:136
  127.0 18.4 %all-to-all-done.1 = bf16[128,2,1024]{2,1,0:T(2,128)(2,1)} async-done(((bf16[128,2,1024]{2,1,0:T(2,128)(2,1)}), bf16[128,2,1024]{2,1,0:T(2,128)(2,1)}, u32[]{:S(2)}, u32[]{:S(2)}) %all-to-all-start.1) | async-done | bytes 524320 | tf_op jit(solution)/shard_map/all_to_all | solution.py:136
  145.4 4.3 %reshape.611 = bf16[512,1,512]{2,1,0:T(2,128)(2,1)} reshape(bf16[128,2,1024]{2,1,0:T(2,128)(2,1)} %all-to-all-done.1) | data formatting | bytes 1048576
  149.8 2.3 convert_bitcast_fusion
  152.8 4.6 %all_to_all.44 = bf16[2,4,4096]{2,1,0:T(4,128)(2,1)S(1)} all-to-all(bf16[2,4,4096]{2,1,0:T(4,128)(2,1)S(1)} %broadcast_in_dim.275), channel_id=1, replica_groups=mesh['groups'=2,'expert'=64,'replica'=2] {'replica'}, dimensions={0} | all-to-all | bytes 131072 | tf_op jit(solution)/shard_map/all_to_all | solution.py:19
  157.4 1.5 convolution_convert_fusion.1
  158.9 2.5 %reshape.598 = bf16[64,2,4096]{2,1,0:T(2,128)(2,1)} reshape(bf16[128,4096]{1,0:T(8,128)(2,1)} %convolution_convert_fusion.1) | data formatting | bytes 2097152 | tf_op jit(solution)/shard_map/reshape | solution.py:171
  161.4 33.8 %all_to_all.45 = bf16[64,2,4096]{2,1,0:T(2,128)(2,1)} all-to-all(bf16[64,2,4096]{2,1,0:T(2,128)(2,1)} %reshape.598), channel_id=1, replica_groups=mesh['groups'=2,'expert'=64,'replica'=2] {'expert'}, dimensions={0} | all-to-all | bytes 2097152 | tf_op jit(solution)/shard_map/all_to_all | solution.py:174
  195.2 2.2 reshape.599
  197.5 3.1 %fusion.3 = f32[128,384]{1,0:T(8,128)S(1)} fusion(bf16[128,4096]{1,0:T(8,128)(2,1)} %reshape.599, bf16[1,4096,384]{2,1,0:T(8,128)(2,1)} %param.25), kind=kOutput, calls=%fused_computation.6 | convolution fusion | flops 402653184 | bytes 4390912 | tf_op jit(solution)/shard_map/dot_general | solution.py:178
  200.9 0.7 fusion.10
  201.7 0.7 convolution_convert_fusion
  202.4 1.1 copy.34
  203.5 35.5 %all_to_all.46 = bf16[64,2,4096]{2,1,0:T(2,128)(2,1)} all-to-all(bf16[64,2,4096]{2,1,0:T(2,128)(2,1)S(1)} %copy.34), channel_id=1, replica_groups=mesh['groups'=2,'expert'=64,'replica'=2] {'expert'}, dimensions={0} | all-to-all | bytes 2097152 | tf_op jit(solution)/shard_map/all_to_all | solution.py:184
  239.0 2.3 reshape.600
  241.3 1.5 fusion.27
  242.8 7.6 %all_to_all.47 = bf16[2,4,4096]{2,1,0:T(4,128)(2,1)S(1)} all-to-all(bf16[2,4,4096]{2,1,0:T(4,128)(2,1)S(1)} %reshape.601), channel_id=1, replica_groups=mesh['groups'=2,'expert'=64,'replica'=2] {'replica'}, dimensions={0} | all-to-all | bytes 131072 | tf_op jit(solution)/shard_map/all_to_all | solution.py:41
  250.4 0.6 add_convert_fusion
  (61 shorter events, 3.0 us)
Async XLA Ops:
  0.0 201.7 %copy-start = (bf16[1,384,4096]{2,1,0:T(8,128)(2,1)S(1)}, bf16[1,384,4096]{2,1,0:T(8,128)(2,1)}, u32[]{:S(2)}) copy-start(bf16[1,384,4096]{2,1,0:T(8,128)(2,1)} %param.27) | copy-start | bytes 9437188
  7.9 92.4 %all-to-all-start = ((bf16[4,128,512]{2,0,1:T(4,128)(2,1)}), bf16[4,128,512]{2,0,1:T(4,128)(2,1)}, u32[]{:S(2)}, u32[]{:S(2)}) async-start(bf16[4,128,512]{2,0,1:T(4,128)(2,1)} %bitcast.68), calls=%async_computation | async-start | bytes 1048576 | tf_op jit(solution)/shard_map/all_to_all | solution.py:130
  38.5 13.0 %collective-permute-start = (bf16[64,512]{1,0:T(8,128)(2,1)}, bf16[64,512]{1,0:T(8,128)(2,1)S(1)}, u32[]{:S(2)}, u32[]{:S(2)}) collective-permute-start(bf16[64,512]{1,0:T(8,128)(2,1)} %get-tuple-element.7), channel_id=1, source_target_pairs={{0,7},{1,8},{2,9},{3,10},{4,11},{5,12},{6,13},{7,14},{8,15},{9,16}... | collective-permute-start | bytes 196616 | tf_op jit(solution)/shard_map/ppermute | solution.py:14
  46.1 15.7 %collective-permute-start.12 = (bf16[64,512]{1,0:T(8,128)(2,1)}, bf16[64,512]{1,0:T(8,128)(2,1)}, u32[]{:S(2)}, u32[]{:S(2)}) collective-permute-start(bf16[64,512]{1,0:T(8,128)(2,1)} %get-tuple-element.8), channel_id=1, source_target_pairs={{6,0},{7,1},{8,2},{9,3},{10,4},{11,5},{12,6},{13,7},{14,8},{15,9},... | collective-permute-start | bytes 196616 | tf_op jit(solution)/shard_map/ppermute | solution.py:14
  47.4 16.3 %collective-permute-start.11 = (bf16[64,512]{1,0:T(8,128)(2,1)}, bf16[64,512]{1,0:T(8,128)(2,1)}, u32[]{:S(2)}, u32[]{:S(2)}) collective-permute-start(bf16[64,512]{1,0:T(8,128)(2,1)} %get-tuple-element.9), channel_id=1, source_target_pairs={{5,0},{6,1},{7,2},{8,3},{9,4},{10,5},{11,6},{12,7},{13,8},{14,9},{... | collective-permute-start | bytes 196616 | tf_op jit(solution)/shard_map/ppermute | solution.py:14
  48.7 18.7 %collective-permute-start.10 = (bf16[64,512]{1,0:T(8,128)(2,1)}, bf16[64,512]{1,0:T(8,128)(2,1)}, u32[]{:S(2)}, u32[]{:S(2)}) collective-permute-start(bf16[64,512]{1,0:T(8,128)(2,1)} %get-tuple-element.10), channel_id=1, source_target_pairs={{4,0},{5,1},{6,2},{7,3},{8,4},{9,5},{10,6},{11,7},{12,8},{13,9},{1... | collective-permute-start | bytes 196616 | tf_op jit(solution)/shard_map/ppermute | solution.py:14
  50.0 18.7 %collective-permute-start.9 = (bf16[64,512]{1,0:T(8,128)(2,1)}, bf16[64,512]{1,0:T(8,128)(2,1)}, u32[]{:S(2)}, u32[]{:S(2)}) collective-permute-start(bf16[64,512]{1,0:T(8,128)(2,1)} %get-tuple-element.11), channel_id=1, source_target_pairs={{3,0},{4,1},{5,2},{6,3},{7,4},{8,5},{9,6},{10,7},{11,8},{12,9},{13... | collective-permute-start | bytes 196616 | tf_op jit(solution)/shard_map/ppermute | solution.py:14
  51.5 20.0 %collective-permute-start.8 = (bf16[64,512]{1,0:T(8,128)(2,1)}, bf16[64,512]{1,0:T(8,128)(2,1)S(1)}, u32[]{:S(2)}, u32[]{:S(2)}) collective-permute-start(bf16[64,512]{1,0:T(8,128)(2,1)} %get-tuple-element.12), channel_id=1, source_target_pairs={{2,0},{3,1},{4,2},{5,3},{6,4},{7,5},{8,6},{9,7},{10,8},{11,9},{12,... | collective-permute-start | bytes 196616 | tf_op jit(solution)/shard_map/ppermute | solution.py:14
  61.8 12.2 %collective-permute-start.7 = (bf16[64,512]{1,0:T(8,128)(2,1)}, bf16[64,512]{1,0:T(8,128)(2,1)S(1)}, u32[]{:S(2)}, u32[]{:S(2)}) collective-permute-start(bf16[64,512]{1,0:T(8,128)(2,1)} %get-tuple-element.13), channel_id=1, source_target_pairs={{1,0},{2,1},{3,2},{4,3},{5,4},{6,5},{7,6},{8,7},{9,8},{10,9},{11,1... | collective-permute-start | bytes 196616 | tf_op jit(solution)/shard_map/ppermute | solution.py:14
  63.7 19.0 %collective-permute-start.6 = (bf16[64,512]{1,0:T(8,128)(2,1)}, bf16[64,512]{1,0:T(8,128)(2,1)S(1)}, u32[]{:S(2)}, u32[]{:S(2)}) collective-permute-start(bf16[64,512]{1,0:T(8,128)(2,1)} %get-tuple-element.14), channel_id=1, source_target_pairs={{0,1},{1,2},{2,3},{3,4},{4,5},{5,6},{6,7},{7,8},{8,9},{9,10},{10,1... | collective-permute-start | bytes 196616 | tf_op jit(solution)/shard_map/ppermute | solution.py:14
  67.4 20.2 %collective-permute-start.5 = (bf16[64,512]{1,0:T(8,128)(2,1)}, bf16[64,512]{1,0:T(8,128)(2,1)S(1)}, u32[]{:S(2)}, u32[]{:S(2)}) collective-permute-start(bf16[64,512]{1,0:T(8,128)(2,1)} %get-tuple-element.15), channel_id=1, source_target_pairs={{0,2},{1,3},{2,4},{3,5},{4,6},{5,7},{6,8},{7,9},{8,10},{9,11},{10,... | collective-permute-start | bytes 196616 | tf_op jit(solution)/shard_map/ppermute | solution.py:14
  68.8 20.2 %collective-permute-start.4 = (bf16[64,512]{1,0:T(8,128)(2,1)}, bf16[64,512]{1,0:T(8,128)(2,1)S(1)}, u32[]{:S(2)}, u32[]{:S(2)}) collective-permute-start(bf16[64,512]{1,0:T(8,128)(2,1)} %get-tuple-element.16), channel_id=1, source_target_pairs={{0,3},{1,4},{2,5},{3,6},{4,7},{5,8},{6,9},{7,10},{8,11},{9,12},{10... | collective-permute-start | bytes 196616 | tf_op jit(solution)/shard_map/ppermute | solution.py:14
  71.5 17.5 %collective-permute-start.3 = (bf16[64,512]{1,0:T(8,128)(2,1)S(1)}, bf16[64,512]{1,0:T(8,128)(2,1)S(1)}, u32[]{:S(2)}, u32[]{:S(2)}) collective-permute-start(bf16[64,512]{1,0:T(8,128)(2,1)S(1)} %get-tuple-element.17), channel_id=1, source_target_pairs={{0,4},{1,5},{2,6},{3,7},{4,8},{5,9},{6,10},{7,11},{8,12},{9,13},{1... | collective-permute-start | bytes 196616 | tf_op jit(solution)/shard_map/ppermute | solution.py:14
  74.0 15.1 %collective-permute-start.2 = (bf16[64,512]{1,0:T(8,128)(2,1)S(1)}, bf16[64,512]{1,0:T(8,128)(2,1)S(1)}, u32[]{:S(2)}, u32[]{:S(2)}) collective-permute-start(bf16[64,512]{1,0:T(8,128)(2,1)S(1)} %get-tuple-element.18), channel_id=1, source_target_pairs={{0,5},{1,6},{2,7},{3,8},{4,9},{5,10},{6,11},{7,12},{8,13},{9,14},{... | collective-permute-start | bytes 196616 | tf_op jit(solution)/shard_map/ppermute | solution.py:14
  82.8 6.3 %collective-permute-start.1 = (bf16[64,512]{1,0:T(8,128)(2,1)S(1)}, bf16[64,512]{1,0:T(8,128)(2,1)S(1)}, u32[]{:S(2)}, u32[]{:S(2)}) collective-permute-start(bf16[64,512]{1,0:T(8,128)(2,1)S(1)} %get-tuple-element.19), channel_id=1, source_target_pairs={{0,6},{1,7},{2,8},{3,9},{4,10},{5,11},{6,12},{7,13},{8,14},{9,15},... | collective-permute-start | bytes 196616 | tf_op jit(solution)/shard_map/ppermute | solution.py:14
  87.7 10.2 %collective-permute-start.13 = (bf16[64,512]{1,0:T(8,128)(2,1)S(1)}, bf16[64,512]{1,0:T(8,128)(2,1)S(1)}, u32[]{:S(2)}, u32[]{:S(2)}) collective-permute-start(bf16[64,512]{1,0:T(8,128)(2,1)S(1)} %get-tuple-element.21), channel_id=1, source_target_pairs={{7,0},{8,1},{9,2},{10,3},{11,4},{12,5},{13,6},{14,7},{15,8},{16,9}... | collective-permute-start | bytes 196616 | tf_op jit(solution)/shard_map/ppermute | solution.py:14
  100.3 26.0 %copy-start.3 = (s32[8,8]{1,0:T(8,128)S(1)}, s32[8,8]{1,0:T(8,128)}, u32[]{:S(2)}) copy-start(s32[8,8]{1,0:T(8,128)} %param.23) | copy-start | bytes 772
  100.3 26.3 %copy-start.5 = (bf16[4096]{0:T(1024)(128)(2,1)S(1)}, bf16[4096]{0:T(1024)(128)(2,1)}, u32[]{:S(2)}) copy-start(bf16[4096]{0:T(1024)(128)(2,1)} %param.22) | copy-start | bytes 24580
  100.3 26.4 %copy-start.4 = (f32[8,8]{1,0:T(8,128)S(1)}, f32[8,8]{1,0:T(8,128)}, u32[]{:S(2)}) copy-start(f32[8,8]{1,0:T(8,128)} %param.24) | copy-start | bytes 772
  110.1 35.3 %all-to-all-start.1 = ((bf16[128,2,1024]{2,1,0:T(2,128)(2,1)}), bf16[128,2,1024]{2,1,0:T(2,128)(2,1)}, u32[]{:S(2)}, u32[]{:S(2)}) async-start(bf16[128,2,1024]{2,1,0:T(2,128)(2,1)} %reshape.610), calls=%async_computation.1 | async-start | bytes 1048576 | tf_op jit(solution)/shard_map/all_to_all | solution.py:136
  127.0 25.5 %copy-start.2 = (bf16[4,4096]{1,0:T(4,128)(2,1)S(1)}, bf16[4,4096]{1,0:T(4,128)(2,1)}, u32[]{:S(2)}) copy-start(bf16[4,4096]{1,0:T(4,128)(2,1)} %param.20) | copy-start | bytes 98308
  197.5 3.1 %copy-start.1 = (bf16[128,4096]{1,0:T(8,128)(2,1)S(1)}, bf16[128,4096]{1,0:T(8,128)(2,1)}, u32[]{:S(2)}) copy-start(bf16[128,4096]{1,0:T(8,128)(2,1)} %reshape.599) | copy-start | bytes 3145732
  197.5 3.5 %copy-start.6 = (bf16[1,4096,384]{2,1,0:T(8,128)(2,1)S(1)}, bf16[1,4096,384]{2,1,0:T(8,128)(2,1)}, u32[]{:S(2)}) copy-start(bf16[1,4096,384]{2,1,0:T(8,128)(2,1)} %param.26) | copy-start | bytes 9437188
where the time goes:
time: 253 us; the launch traced here: 251 us
  starting transfers between devices  85.4 us (34%)
  blocking collectives  81.4 us (32%)
  waiting for transfers between devices  36.3 us (14%)
  local copies, waits for them, and re-layouts  23.7 us (9%)
  matrix products  13.3 us (5%)
  other arithmetic  10.2 us (4%)
    ppermute x14, starting transfers between devices, shifted(): return lax.ppermute(block, axis, route)  41.2 us
    all_to_all x1, blocking collectives, on_device(): lax.all_to_all(partial_value.astype(jnp.bfloat16), 'expert', split_axis=0...  35.5 us
    all_to_all x1, blocking collectives, on_device(): lax.all_to_all(outgoing, 'expert', split_axis=0, concat_axis=0, tiled=True)  33.8 us
    all_to_all x1, starting transfers between devices, on_device(): lax.all_to_all(repeated, ('expert', 'replica'), split_axis=1, concat_axis...  28.1 us
    all_to_all x1, waiting for transfers between devices, on_device(): lax.all_to_all(partial_cols.astype(jnp.bfloat16), ('expert', 'replica'),...  18.4 us
    ppermute x14, waiting for transfers between devices, shifted(): return lax.ppermute(block, axis, route)  17.8 us
    all_to_all x1, starting transfers between devices, on_device(): lax.all_to_all(partial_cols.astype(jnp.bfloat16), ('expert', 'replica'),...  16.1 us
    unnamed x18, local copies, waits for them, and re-layouts  8.05 us
  transfers between devices with their start and end apart: 16, of which 3 were waited for; matrix products, arithmetic and copies ran while one was open for 2% of the time, Pallas kernels for 0%

commit v1 on v0

v1 whole, which is shorter than its diff:
```python
import functools
import math

import jax
import jax.numpy as jnp
from jax import lax
from jax.experimental import pallas as pl
from jax.experimental.pallas import tpu as pltpu
from jax.sharding import PartitionSpec as P

HW = 128
SLOTS = 2
BF = jnp.bfloat16
F32 = jnp.float32
NEG = -jnp.inf


def dot(a, b, dims=((1,), (0,)), precision=None):
    return lax.dot_general(a, b, (dims, ((), ())), preferred_element_type=F32, precision=precision)


def iota(shape, dim):
    return lax.broadcasted_iota(jnp.int32, shape, dim)


def kernel(
    n, q_hbm, tk_hbm, tv_hbm, k_hbm, v_hbm, len_hbm, res_hbm, ow_hbm, gain_hbm, ids_hbm, rw_hbm, wg_hbm, wu_hbm, wd_hbm,
    out_ref,
    q_s, tk_s, tv_s, k_s, v_s, len_s, gain_s, ids_s, rw_s, wgu, wdo, wdp,
    wb, res, att, xs, ysend, rbuf, hid, hg, hm, hall, tsend, town, toth,
    idt, id1, idg, id2, pbuf, ctb, ss0, ss1, ss2t, ss2, sso, ssp,
    acco, accx, scr, acto, acts, actx, osend, gbuf, csend, zbuf, fsend, frecv,
    lsem, ssem, wsem, rsem, tsem1, xsem, rrsem, hmsem, hsem, tsem, osem, ss1sem, ss2sem, id1sem, id2sem, dsem, gsem, zsem,
):
    r = lax.axis_index("replica")
    e = lax.axis_index("expert")
    x, y = e // n, e % n
    u, v = x * (1 - r) + y * r, y * (1 - r) + x * r
    a, b = n - r * (n - 1), 1 + r * (n - 1)
    heads = n * n
    cols = wb.shape[3]
    half = n * cols
    lanes = 2 * HW

    def own(uu, vv):
        return {"expert": uu * a + vv * b, "replica": r}

    partner = {"expert": e, "replica": 1 - r}

    def remote(src, dst, send, recv, device):
        return pltpu.make_async_remote_copy(
            src, dst, ssem.at[send], recv, device_id=device, device_id_type=pl.DeviceIdType.MESH
        )

    def local(src, dst, sem):
        return pltpu.make_async_copy(src, dst, sem)

    def arrived(ref, sem):
        local(ref, ref, sem).wait()

    def around(w, d):
        return lax.rem(w + d, n)

    scope = jax.named_scope

    with scope("barrier"):
        bar = pltpu.get_barrier_semaphore()

        def greet(d, c):
            for rr in (0, 1):
                pl.semaphore_signal(bar, device_id={"expert": around(x, d) * n + y, "replica": rr}, device_id_type=pl.DeviceIdType.MESH)
                pl.semaphore_signal(bar, device_id={"expert": x * n + around(y, d), "replica": rr}, device_id_type=pl.DeviceIdType.MESH)
            return c

        lax.fori_loop(1, n, greet, 0)
        pl.semaphore_signal(bar, device_id=partner, device_id_type=pl.DeviceIdType.MESH)

        def qcopy(h, c):
            local(q_hbm.at[:, pl.ds(pl.multiple_of(h * HW, HW), HW)], q_s.at[h], lsem.at[0]).start()
            return c

        lax.fori_loop(0, heads, qcopy, 0)
        local(len_hbm, len_s, lsem.at[1]).start()
        local(tk_hbm, tk_s, lsem.at[2]).start()
        local(tv_hbm, tv_s, lsem.at[3]).start()
        local(ids_hbm, ids_s, lsem.at[4]).start()
        local(rw_hbm, rw_s, lsem.at[5]).start()
        local(k_hbm, k_s, lsem.at[6]).start()
        local(v_hbm, v_s, lsem.at[7]).start()
        local(gain_hbm, gain_s, lsem.at[8]).start()
        local(ow_hbm.at[:, pl.ds(pl.multiple_of(r * half + v * cols, cols), cols)], wb.at[v, r], lsem.at[9]).start()
        local(res_hbm.at[:, pl.ds(pl.multiple_of(r * half + v * cols, cols), cols)], res.at[v, r], lsem.at[10]).start()
        hidden_units = wg_hbm.shape[2]
        local(wg_hbm.at[0], wgu.at[:, pl.ds(0, hidden_units)], lsem.at[11]).start()
        local(wu_hbm.at[0], wgu.at[:, pl.ds(hidden_units, hidden_units)], lsem.at[12]).start()
        local(wd_hbm.at[0, :, pl.ds(pl.multiple_of(r * half, half), half)], wdo, lsem.at[13]).start()
        pl.semaphore_wait(bar, 4 * (n - 1) + 1)

    with scope("weights_send"):

        def wsend(d, c):
            vv = around(v, d)
            at = pl.ds(pl.multiple_of(r * half + vv * cols, cols), cols)
            remote(ow_hbm.at[:, at], wb.at[v, r], 0, wsem.at[0], own(u, vv)).start()
            return c

        def wcross(d, c):
            uu = around(u, d)
            at = pl.ds(pl.multiple_of((1 - r) * half + uu * cols, cols), cols)
            remote(ow_hbm.at[:, at], wb.at[u, r], 1, wsem.at[1], {"expert": uu * a + v * b, "replica": 1 - r}).start()
            return c

        def rsend(d, c):
            vv = around(v, d)
            at = pl.ds(pl.multiple_of(r * half + vv * cols, cols), cols)
            remote(res_hbm.at[:, at], res.at[v, r], 2, rsem.at[0], own(u, vv)).start()
            return c

        def rcross(d, c):
            uu = around(u, d)
            at = pl.ds(pl.multiple_of((1 - r) * half + uu * cols, cols), cols)
            remote(res_hbm.at[:, at], res.at[u, r], 3, rsem.at[1], {"expert": uu * a + v * b, "replica": 1 - r}).start()
            return c

        lax.fori_loop(1, n, wsend, 0)
        lax.fori_loop(0, n, wcross, 0)
        lax.fori_loop(1, n, rsend, 0)
        lax.fori_loop(0, n, rcross, 0)
        remote(wd_hbm.at[0, :, pl.ds(pl.multiple_of((1 - r) * half, half), half)], wdp, 4, dsem.at[0], partner).start()

    tok = ids_s.shape[0]
    topk = ids_s.shape[1]
    tokens = n * tok
    with scope("ids_send"):
        local(ids_hbm, ids_s, lsem.at[4]).wait()
        local(rw_hbm, rw_s, lsem.at[5]).wait()
        weight = rw_s[...]
        mixing = weight / jnp.sum(weight, axis=1, keepdims=True)
        lane = iota((tok, HW), 1)
        row = iota((tok, HW), 0)
        place = (lane == v * tok + row).astype(F32)
        place_mix = (lane == tokens + v * tok + row).astype(F32)
        exact = lax.Precision.HIGHEST
        idt[...] = dot(ids_s[...].astype(F32), place, ((0,), (0,)), exact) + dot(mixing, place_mix, ((0,), (0,)), exact)

        def id1send(d, c):
            remote(idt, id1.at[v], 5, id1sem, own(u, around(v, d))).start()
            return c

        lax.fori_loop(1, n, id1send, 0)
        id1[v] = idt[...]

    with scope("attention"):
        seqs = k_s.shape[0]
        pos = k_s.shape[1]
        kvh = k_s.shape[2] // HW
        per = heads // kvh
        rows = per * seqs
        arrived(q_s, lsem.at[0])
        local(len_hbm, len_s, lsem.at[1]).wait()
        local(tk_hbm, tk_s, lsem.at[2]).wait()
        local(tv_hbm, tv_s, lsem.at[3]).wait()
        local(k_hbm, k_s, lsem.at[6]).wait()
        inv_root = 1.0 / math.sqrt(HW)
        rowseq = lax.rem(iota((rows, pos), 0), seqs)
        colpos = iota((rows, pos), 1)
        visible = jnp.concatenate(
            [jnp.where((rowseq == s) & (colpos < len_s[s]), 0.0, NEG) for s in range(seqs)], axis=1
        )
        fresh_ok = lax.rem(iota((rows, seqs), 0), seqs) == iota((rows, seqs), 1)
        for g in range(kvh):
            at = slice(g * HW, (g + 1) * HW)
            qg = q_s[g * per : (g + 1) * per].reshape(rows, HW)
            kg = k_s[:, :, at].reshape(seqs * pos, HW)
            s_old = dot(qg, kg, ((1,), (1,))) * inv_root + visible
            s_new = jnp.where(fresh_ok, dot(qg, tk_s[:, at], ((1,), (1,))) * inv_root, NEG)
            top = jnp.maximum(jnp.max(s_old, axis=1, keepdims=True), jnp.max(s_new, axis=1, keepdims=True))
            p_old = jnp.exp(s_old - top)
            p_new = jnp.exp(s_new - top)
            scale = 1.0 / (jnp.sum(p_old, axis=1, keepdims=True) + jnp.sum(p_new, axis=1, keepdims=True))
            p_old = (p_old * scale).astype(BF)
            p_new = (p_new * scale).astype(BF).astype(F32)
            if g == 0:
                local(v_hbm, v_s, lsem.at[7]).wait()
            vg = v_s[:, :, at].reshape(seqs * pos, HW)
            mixed = dot(p_old, vg)
            tv = tv_s[:, at].astype(F32)
            for s in range(seqs):
                mixed = mixed + p_new[:, s : s + 1] * tv[s : s + 1, :]
            att[g * (n // kvh) : (g + 1) * (n // kvh)] = mixed.astype(BF).reshape(n // kvh, n, seqs, HW)

    with scope("feature_send"):

        def t1send(d, c):
            xx, yy = around(x, d), around(y, d)
            remote(att.at[xx], xs.at[y, :, pl.ds((x * 2 + r) * seqs, seqs)], 7, tsem1, {"expert": xx * n + y, "replica": 0}).start()
            remote(att.at[:, yy], xs.at[x, :, pl.ds((y * 2 + r) * seqs, seqs)], 7, tsem1, {"expert": x * n + yy, "replica": 1}).start()
            return c

        lax.fori_loop(1, n, t1send, 0)

        @pl.when(r == 0)
        def _():
            remote(att.at[:, y], xs.at[x, :, pl.ds((y * 2 + r) * seqs, seqs)], 7, tsem1, partner).start()
            local(att.at[x], xs.at[y, :, pl.ds((x * 2 + r) * seqs, seqs)], lsem.at[14]).start()

        @pl.when(r == 1)
        def _():
            remote(att.at[x], xs.at[y, :, pl.ds((x * 2 + r) * seqs, seqs)], 7, tsem1, partner).start()
            local(att.at[:, y], xs.at[x, :, pl.ds((y * 2 + r) * seqs, seqs)], lsem.at[14]).start()

    with scope("ids_second"):
        arrived(id1.at[pl.ds(0, n - 1)], id1sem)
        idg[...] = functools.reduce(lambda p, q: p + q, [id1[i] for i in range(n)])

        def id2send(d, c):
            remote(idg, id2.at[u], 6, id2sem, own(around(u, d), v)).start()
            return c

        lax.fori_loop(1, n, id2send, 0)
        id2[u] = idg[...]

    with scope("feature_gather"):
        arrived(att.at[0], lsem.at[14])
        arrived(xs.at[0, :, pl.ds(0, (2 * n - 1) * seqs)], tsem1)

        def t2send(d, c):
            remote(xs.at[v], xs.at[v], 8, xsem.at[v], own(u, around(v, d))).start()
            return c

        lax.fori_loop(1, n, t2send, 0)

    with scope("tables"):
        arrived(id2.at[pl.ds(0, n - 1)], id2sem)
        block = (iota((n, HW), 1) // tok == iota((n, HW), 0)).astype(F32)
        before = (
            (iota((HW, HW), 0) // tok == iota((HW, HW), 1) // tok) & (iota((HW, HW), 0) < iota((HW, HW), 1))
        ).astype(BF)
        place_v = iota((n, 1), 0).astype(F32)
        ue = u.astype(F32)
        ve = v.astype(F32)
        ae = a.astype(F32)
        be = b.astype(F32)
        expert_v = ae * ue + be * place_v
        named = []
        for i in range(n):
            got = id2[i]
            named.append(functools.reduce(lambda p, q: p + q, [(got[k : k + 1] == expert_v).astype(F32) for k in range(topk)]))
        named = jnp.concatenate(named, axis=0)
        rank = dot(named.astype(BF), before)
        for i in range(n):
            here = slice(i * n, (i + 1) * n)
            picks = []
            for j in range(SLOTS):
                hit = jnp.where(rank[here] == j, named[here], 0.0)
                picks.append(hit[:, None, :] * block[None])
            pbuf[i] = jnp.stack(picks, axis=1).reshape(HW, HW).astype(BF)
        got = idg[...]
        back = pltpu.roll(got, tokens, 1)
        expert_u = ae * place_v + be * ve
        same = [got[k : k + 1] == expert_u for k in range(topk)]
        chosen = functools.reduce(lambda p, q: p + q, [s.astype(F32) for s in same])
        mix = functools.reduce(lambda p, q: p + q, [jnp.where(s, back[k : k + 1], 0.0) for k, s in enumerate(same)])
        rank = dot(jnp.concatenate([chosen, chosen], axis=0).astype(BF), before)[:n]
        picks = []
        for j in range(SLOTS):
            hit = jnp.where(rank == j, mix, 0.0)
            picks.append(hit[:, None, :] * block[None])
        table = jnp.stack(picks, axis=1).reshape(HW, HW)
        high = table.astype(BF)
        low = (table - high.astype(F32)).astype(BF)
        ctb[...] = jnp.concatenate([high[:, :tokens], low[:, :tokens]], axis=1)

    with scope("project"):
        local(ow_hbm.at[:, pl.ds(0, cols)], wb.at[v, r], lsem.at[9]).wait()
        arrived(wb.at[pl.ds(0, n - 1), 0], wsem.at[0])
        arrived(wb.at[:, 0], wsem.at[1])
        wv = wb.reshape(n * HW, cols)

        def project(i, c):
            odd = lax.rem(i, 2)
            d = odd * ((i + 1) // 2) + (1 - odd) * (n - i // 2)
            vv = around(v, d)

            @pl.when(i > 0)
            def _():
                arrived(xs.at[vv], xsem.at[vv])

            lhs = jnp.concatenate([xs[vv, k] for k in range(n)], axis=1)
            part = dot(lhs, wv[...])
            ysend[:, vv] = part.astype(BF).reshape(n, tok, cols)
            return c

        lax.fori_loop(0, n, project, 0)

    with scope("reduce_send"):

        def ysend_to(d, c):
            uu = around(u, d)
            remote(ysend.at[uu], rbuf.at[u], 9, rrsem, own(uu, v)).start()
            return c

        lax.fori_loop(1, n, ysend_to, 0)
        rbuf[u] = ysend[u]
        local(res_hbm.at[:, pl.ds(0, cols)], res.at[v, r], lsem.at[10]).wait()
        arrived(res.at[pl.ds(0, n - 1), 0], rsem.at[0])
        arrived(res.at[:, 0], rsem.at[1])
        local(gain_hbm, gain_s, lsem.at[8]).wait()
    with scope("reduce_wait"):
        arrived(rbuf.at[pl.ds(0, n - 1)], rrsem)
    with scope("hidden"):
        total = res[...].astype(F32).reshape(n * tok, cols)
        for i in range(n):
            total = total + rbuf[i].astype(F32).reshape(tokens, cols)
        hid[...] = total.reshape(n, tok, cols)
        gain = gain_s[pl.ds(pl.multiple_of(r * half + v * cols, cols), cols)].astype(F32).reshape(1, cols)
        hg[...] = (total * gain).astype(BF)

        def d1send(d, c):
            remote(hg, hall.at[u], 10, hsem.at[u], own(around(u, d), v)).start()
            return c

        lax.fori_loop(1, n, d1send, 0)
        hall[u] = hg[...]
        square = (total * total).astype(BF)
        sums = dot(jnp.ones((n, cols), BF), square, ((1,), (1,)))
        ss0[...] = jnp.concatenate([sums, jnp.zeros((n, HW - tokens), F32)], axis=1)

        def ss1send(d, c):
            vv = around(v, d)
            remote(ss0, ss1.at[v], 11, ss1sem, own(u, vv)).start()
            remote(hid.at[vv], hm.at[v], 12, hmsem, own(u, vv)).start()
            return c

        lax.fori_loop(1, n, ss1send, 0)
        ss1[v] = ss0[...]
        hm[v] = hid[v]

    with scope("dispatch"):

        def pack(i, c):
            odd = lax.rem(i, 2)
            d = odd * ((i + 1) // 2) + (1 - odd) * (n - i // 2)
            uu = around(u, d)

            @pl.when(i > 0)
            def _():
                arrived(hall.at[uu], hsem.at[uu])

            slots = dot(pbuf[uu, :, pl.ds(0, tokens)], hall[uu]).astype(BF)
            tsend[uu] = slots.reshape(n, SLOTS * n, cols)

            def to(dd, cc):
                vv = around(v, dd)
                remote(tsend.at[uu, vv], town.at[v, uu], 13, tsem.at[v], own(u, vv)).start()
                return cc

            lax.fori_loop(1, n, to, 0)
            town[v, uu] = tsend[uu, v]
            return c

        lax.fori_loop(0, n, pack, 0)

    with scope("sums_second"):
        arrived(ss1.at[pl.ds(0, n - 1)], ss1sem)
        ss2t[...] = functools.reduce(lambda p, q: p + q, [ss1[i] for i in range(n)])

        def ss2send(d, c):
            remote(ss2t, ss2.at[u], 14, ss2sem, own(around(u, d), v)).start()
            return c

        lax.fori_loop(1, n, ss2send, 0)
        ss2[u] = ss2t[...]

    with scope("weights_wait"):
        local(wg_hbm.at[0], wgu.at[:, pl.ds(0, hidden_units)], lsem.at[11]).wait()
        local(wu_hbm.at[0], wgu.at[:, pl.ds(0, hidden_units)], lsem.at[12]).wait()
        acco[...] = jnp.zeros_like(acco)
        accx[...] = jnp.zeros_like(accx)
        tiles = accx.shape[0]
        tv_own = town.reshape(n, HW, cols)
        tv_oth = toth.reshape(n, HW, cols)
    with scope("gate_up_own"):

        def gate_own(i, c):
            odd = lax.rem(i, 2)
            d = odd * ((i + 1) // 2) + (1 - odd) * (n - i // 2)
            vv = around(v, d)

            @pl.when(i > 0)
            def _():
                arrived(town.at[vv], tsem.at[vv])

            remote(town.at[vv], toth.at[i], 15, osem.at[i], partner).start()
            at = pl.ds(pl.multiple_of(r * half + vv * cols, cols), cols)
            acco[...] += dot(tv_own[vv], wgu[at, :])
            return c

        lax.fori_loop(0, n, gate_own, 0)
    with scope("gate_up_other"):

        def gate_other(i, c):
            odd = lax.rem(i, 2)
            d = odd * ((i + 1) // 2) + (1 - odd) * (n - i // 2)
            uu = around(u, d)
            arrived(toth.at[i], osem.at[i])
            at = pl.ds(pl.multiple_of((1 - r) * half + uu * cols, cols), cols)
            part = dot(tv_oth[i], wgu[at, :])
            for t in range(tiles):
                accx[t] += part[:, t * HW : (t + 1) * HW]
            return c

        lax.fori_loop(0, n, gate_other, 0)

    with scope("sums_third"):
        arrived(ss2.at[pl.ds(0, n - 1)], ss2sem)
        for i in range(n):
            mine = pbuf[i, pl.ds(pl.multiple_of(v * SLOTS * n, SLOTS * n), SLOTS * n), :].astype(F32)
            column = jnp.sum(mine * ss2[i][0:1], axis=1, keepdims=True)
            sso[i * SLOTS * n : (i + 1) * SLOTS * n, :] = jnp.broadcast_to(column, (SLOTS * n, HW))
        remote(sso, ssp, 16, dsem.at[1], partner).start()
        arrived(ssp, dsem.at[1])

    with scope("activation"):

        def swapped(ref):
            return jnp.concatenate(
                [ref[pl.ds(j * n + i, n, stride=SLOTS * n), :] for i in range(n) for j in range(SLOTS)], axis=0
            )

        model = 2 * half
        scale = lax.rsqrt((sso[...] + swapped(ssp)) * (1.0 / model) + 1e-06)
        up_at = tiles // 2
        for t in range(up_at):
            gate = (acco[:, t * HW : (t + 1) * HW] + swapped(accx.at[t])) * scale
            up = (acco[:, (t + up_at) * HW : (t + up_at + 1) * HW] + swapped(accx.at[t + up_at])) * scale
            act = gate / (1.0 + jnp.exp(-gate)) * up
            acto[:, t * HW : (t + 1) * HW] = act.astype(BF)
            scr[t] = act
        for t in range(up_at):
            acts[:, t * HW : (t + 1) * HW] = swapped(scr.at[t]).astype(BF)
        remote(acts, actx, 17, dsem.at[2], partner).start()
        local(wd_hbm.at[0, :, pl.ds(0, half)], wdo, lsem.at[13]).wait()
        arrived(wdp, dsem.at[0])
        arrived(actx, dsem.at[2])

    with scope("down"):
        osv = osend.reshape(HW, half)

        def down(i, c):
            at = pl.ds(pl.multiple_of(i * cols, cols), cols)
            osv[:, at] = (dot(acto[...], wdo[:, at]) + dot(actx[...], wdp[:, at])).astype(BF)
            return c

        lax.fori_loop(0, n, down, 0)

        def gsend(d, c):
            uu = around(u, d)
            remote(osend.at[uu], gbuf.at[u], 18, gsem, own(uu, v)).start()
            return c

        lax.fori_loop(1, n, gsend, 0)
        gbuf[u] = osend[u]
    with scope("return_wait"):
        arrived(gbuf.at[pl.ds(0, n - 1)], gsem)
    with scope("combine"):
        gv = gbuf.reshape(HW, half)

        def combine(i, c):
            at = pl.ds(pl.multiple_of(i * cols, cols), cols)
            both = dot(ctb[...], gv[:, at], ((0,), (0,)))
            csend[:, :, at] = (both[:tokens] + both[tokens:]).astype(BF).reshape(n, tok, cols)
            return c

        lax.fori_loop(0, n, combine, 0)

        def zsend(d, c):
            vv = around(v, d)
            remote(csend.at[vv], zbuf.at[v], 19, zsem, own(u, vv)).start()
            return c

        lax.fori_loop(1, n, zsend, 0)
        zbuf[v] = csend[v]
        arrived(hm.at[pl.ds(0, n - 1)], hmsem)
    with scope("home_wait"):
        arrived(zbuf.at[pl.ds(0, n - 1)], zsem)
    with scope("final"):
        mine = tok // 2
        for i in range(n):
            at = slice(i * cols, (i + 1) * cols)
            total = hm[i]
            for j in range(n):
                total = total + zbuf[j, :, at].astype(F32)
            keep = jnp.where(r == 0, total[:mine], total[mine:])
            give = jnp.where(r == 0, total[mine:], total[:mine])
            out_ref[:, pl.ds(pl.multiple_of(r * half + i * cols, cols), cols)] = keep.astype(BF)
            fsend[:, at] = give.astype(BF)
        remote(fsend, frecv, 20, dsem.at[3], partner).start()
        arrived(frecv, dsem.at[3])
        out_ref[:, pl.ds(pl.multiple_of((1 - r) * half, half), half)] = frecv[...]

    with scope("drain"):

        most = pl.ds(0, n - 1)
        for send, ref in enumerate((
            wb.at[most, 0], wb.at[:, 0], res.at[most, 0], res.at[:, 0], wdp, id1.at[most], id2.at[most],
            xs.at[0, :, pl.ds(0, (2 * n - 1) * seqs)], xs.at[most], rbuf.at[most], hall.at[most], ss1.at[most], hm.at[most],
            town.at[most], ss2.at[most], town, sso, acts, gbuf.at[most], zbuf.at[most], fsend,
        )):
            arrived(ref, ssem.at[send])


def solution(mesh):
    n = math.isqrt(mesh.shape["expert"])

    def on_device(queries, token_keys, token_values, stored_keys, stored_values, kv_len, residual, out_weight, norm_gain,
                  expert_ids, route_weight, w_gate, w_up, w_down):
        seqs, pos, kvw = stored_keys.shape
        heads = queries.shape[1] // HW
        model = residual.shape[1]
        half = model // 2
        cols = half // n
        tok, topk = expert_ids.shape
        hidden = w_gate.shape[2]
        tokens = n * tok
        slots = SLOTS * n
        tiles = 2 * hidden // HW
        wrows = out_weight.shape[0]
        vmem = pltpu.VMEM
        dma = pltpu.SemaphoreType.DMA
        scratch = [
            vmem((heads, seqs, HW), BF), vmem((seqs, kvw), BF), vmem((seqs, kvw), BF),
            vmem((seqs, pos, kvw), BF), vmem((seqs, pos, kvw), BF), pltpu.SMEM((seqs,), jnp.int32),
            vmem((model,), BF), vmem((tok, topk), jnp.int32), vmem((tok, topk), F32),
            vmem((model, 2 * hidden), BF), vmem((hidden, half), BF), vmem((hidden, half), BF),
            vmem((n, 2, wrows, cols), BF), vmem((n, 2, seqs, cols), BF),
            vmem((n, n, seqs, HW), BF), vmem((n, n, tokens, HW), BF),
            vmem((n, n, tok, cols), BF), vmem((n, n, tok, cols), BF),
            vmem((n, tok, cols), F32), vmem((tokens, cols), BF), vmem((n, tok, cols), F32),
            vmem((n, tokens, cols), BF), vmem((n, n, slots, cols), BF), vmem((n, n, slots, cols), BF), vmem((n, n, slots, cols), BF),
            vmem((topk, HW), F32), vmem((n, topk, HW), F32), vmem((topk, HW), F32), vmem((n, topk, HW), F32),
            vmem((n, HW, HW), BF), vmem((HW, 2 * tokens), BF),
            vmem((n, HW), F32), vmem((n, n, HW), F32), vmem((n, HW), F32), vmem((n, n, HW), F32),
            vmem((HW, HW), F32), vmem((HW, HW), F32),
            vmem((HW, 2 * hidden), F32), vmem((tiles, HW, HW), F32), vmem((tiles // 2, HW, HW), F32),
            vmem((HW, hidden), BF), vmem((HW, hidden), BF), vmem((HW, hidden), BF),
            vmem((n, slots, half), BF), vmem((n, slots, half), BF),
            vmem((n, tok, half), BF), vmem((n, tok, half), BF), vmem((tok // 2, half), BF), vmem((tok // 2, half), BF),
            dma((15,)), dma((21,)), dma((2,)), dma((2,)), dma, dma((n,)), dma, dma, dma((n,)), dma((n,)), dma((n,)), dma, dma, dma, dma, dma((4,)), dma, dma,
        ]
        return pl.pallas_call(
            functools.partial(kernel, n),
            out_shape=jax.ShapeDtypeStruct(residual.shape, BF),
            in_specs=[pl.BlockSpec(memory_space=pl.ANY)] * 14,
            out_specs=pl.BlockSpec(memory_space=pltpu.VMEM),
            scratch_shapes=scratch,
            compiler_params=pltpu.CompilerParams(
                collective_id=0, has_side_effects=True, vmem_limit_bytes=60 * 1024 * 1024
            ),
        )(queries, token_keys, token_values, stored_keys, stored_values, kv_len, residual, out_weight, norm_gain,
          expert_ids, route_weight, w_gate, w_up, w_down)

    everyone = ("groups", "expert", "replica")
    in_specs = (
        P(everyone, None), P(everyone, None), P(everyone, None), P(everyone, None, None), P(everyone, None, None),
        P(everyone), P(everyone, None), P(("expert", "replica"), None), P(), P(("groups", "expert"), None),
        P(("groups", "expert"), None), P("expert", None, "replica"), P("expert", None, "replica"), P("expert", "replica", None),
    )
    return jax.shard_map(
        on_device, mesh=mesh, in_specs=in_specs, out_specs=P(everyone, None), check_vma=False
    )
```

time: 253 us -> 101 us (0.40)
  Pallas kernels: 0 us -> 99.9 us
  starting transfers between devices: 85.4 us -> 0 us
  blocking collectives: 81.4 us -> 0 us
  waiting for transfers between devices: 36.3 us -> 0 us
  local copies, waits for them, and re-layouts: 23.7 us -> 1.39 us
  matrix products: 13.3 us -> 0 us
  other arithmetic: 10.2 us -> 0 us
    pallas_call x0 -> x1, Pallas kernels: none -> 99.9 us  [on_device(): pl.pallas_call(functools.partial(kernel, n), out_shape=jax.ShapeDtypeStru...]
    all_to_all x4 -> x0, blocking collectives: 81.4 us -> none  [the longest x1 35.5 us: on_device(): lax.all_to_all(partial_value.astype(jnp.bfloat16), 'expert', split_axis=0...]
    all_to_all x2 -> x0, starting transfers between devices: 44.2 us -> none  [the longest x1 28.1 us: on_device(): lax.all_to_all(repeated, ('expert', 'replica'), split_axis=1, concat_axis...]
    ppermute x14 -> x0, starting transfers between devices: 41.2 us -> none  [shifted(): return lax.ppermute(block, axis, route)]
    all_to_all x2 -> x0, waiting for transfers between devices: 18.4 us -> none  [the longest x1 18.4 us: on_device(): lax.all_to_all(partial_cols.astype(jnp.bfloat16), ('expert', 'replica'),...]
    ppermute x14 -> x0, waiting for transfers between devices: 17.8 us -> none  [shifted(): return lax.ppermute(block, axis, route)]
    dot_general x9 -> x0, matrix products: 13.3 us -> none  [the longest x1 3.06 us: on_device(): gate_act = jnp.dot(slot_rows, w_gate[0], preferred_element_type=jnp.float32)]
    reshape x7 -> x0, local copies, waits for them, and re-layouts: 9.88 us -> none  [the longest x1 2.52 us: on_device(): outgoing = outgoing.reshape(expert_count, capacity, -1)]
  transfers between devices with their start and end apart: 16 -> 0, of which waited for: 3 -> 0; matrix products, arithmetic and copies ran while one was open for 2% -> 0% of each run, Pallas kernels for 0% -> 0%
where the time goes in v1:
time: 101 us
  Pallas kernels  99.9 us (99%)
  local copies, waits for them, and re-layouts  1.39 us (1%)
    pallas_call x1, Pallas kernels, on_device(): pl.pallas_call(functools.partial(kernel, n), out_shape=jax.ShapeDtypeStru...  99.9 us

profile of v1, /device:TPU:513, one launch (start us, length us, event | category | flops | bytes accessed | tf_op | source)
XLA Modules:
  0.0 101.3 jit_solution(2769049565600911898)
XLA Ops:
  0.0 99.9 %shard_map.136 = bf16[4,4096]{1,0:T(4,128)(2,1)} custom-call(bf16[4,8192]{1,0:T(4,128)(2,1)} %q_hbm.1, bf16[4,512]{1,0:T(4,128)(2,1)} %tk_hbm.1, bf16[4,512]{1,0:T(4,128)(2,1)} %tv_hbm.1, bf16[4,256,512]{2,1,0:T(8,128)(2,1)} %k_hbm.1, bf16[4,256,512]{2,1,0:T(8,128)(2,1)} %v_hbm.1, s32[4]{0:T(128)} %len_hbm.1, bf16[4,4096]{1,0:T(4,128)(2,1)} %res_hbm.1, ...), custom_call_target="tpu_custom_call" | custom-call | tf_op jit(solution)/shard_map/pallas_call | solution.py:551
  99.9 1.4 %copy.16 = bf16[4,4096]{1,0:T(4,128)(2,1)} copy(bf16[4,4096]{1,0:T(4,128)(2,1)} %shard_map.136) | data formatting | bytes 65536

commit v2 on v1

v2 whole, which is shorter than its diff:
```python
import functools
import math

import jax
import jax.numpy as jnp
from jax import lax
from jax.experimental import pallas as pl
from jax.experimental.pallas import tpu as pltpu
from jax.sharding import PartitionSpec as P

HW = 128
SLOTS = 2
BF = jnp.bfloat16
F32 = jnp.float32
NEG = -jnp.inf


def dot(a, b, dims=((1,), (0,)), precision=None):
    return lax.dot_general(a, b, (dims, ((), ())), preferred_element_type=F32, precision=precision)


def iota(shape, dim):
    return lax.broadcasted_iota(jnp.int32, shape, dim)


def kernel(
    n, q_hbm, tk_hbm, tv_hbm, k_hbm, v_hbm, len_hbm, res_hbm, ow_hbm, gain_hbm, ids_hbm, rw_hbm, wg_hbm, wu_hbm, wd_hbm,
    out_ref,
    q_s, tk_s, tv_s, k_s, v_s, len_s, gain_s, ids_s, rw_s, wgu, wdn,
    wb, res, att, xs, ysend, rbuf, hid, hg, hm, hall, tsend, town, toth,
    idt, id1, idg, id2, pbuf, ctb, ss0, ss1, ss2t, ss2, sso, ssp,
    acco, accx, scr, acto, acts, actx, osend, gbuf, csend, zbuf,
    lsem, ssem, wsem, rsem, t1sem, xsem, rrsem, hmsem, hsem, tsem, osem, ss1sem, ss2sem, id1sem, id2sem, dsem, gsem, zsem,
):
    r = lax.axis_index("replica")
    e = lax.axis_index("expert")
    x, y = e // n, e % n
    u, v = x * (1 - r) + y * r, y * (1 - r) + x * r
    a, b = n - r * (n - 1), 1 + r * (n - 1)
    heads = n * n
    cols = wb.shape[3]
    half = n * cols
    seqs, pos = k_s.shape[0], k_s.shape[1]
    tok, topk = ids_s.shape
    tokens = n * tok
    slots = SLOTS * n
    most = pl.ds(0, n - 1)
    mesh_id = pl.DeviceIdType.MESH

    def own(uu, vv):
        return {"expert": uu * a + vv * b, "replica": r}

    def across(uu, vv):
        return {"expert": uu * a + vv * b, "replica": 1 - r}

    partner = {"expert": e, "replica": 1 - r}

    def remote(src, dst, send, recv, device):
        return pltpu.make_async_remote_copy(src, dst, ssem.at[send], recv, device_id=device, device_id_type=mesh_id)

    def local(src, dst, sem):
        return pltpu.make_async_copy(src, dst, sem)

    def arrived(ref, sem):
        local(ref, ref, sem).wait()

    def around(w, d):
        return lax.rem(w + d, n)

    def far(i):
        return n // 2 + (2 * lax.rem(i, 2) - 1) * (i // 2)

    def each(body):
        def step(i, c):
            body(far(i), c)
            return c

        lax.fori_loop(1, n, step, 0)

    def columns(plane, block):
        return pl.ds(pl.multiple_of(plane * half + block * cols, cols), cols)

    scope = jax.named_scope

    with scope("barrier"):
        bar = pltpu.get_barrier_semaphore()

        def greet(d, c):
            for rr in (0, 1):
                pl.semaphore_signal(bar, device_id={"expert": around(x, d) * n + y, "replica": rr}, device_id_type=mesh_id)
                pl.semaphore_signal(bar, device_id={"expert": x * n + around(y, d), "replica": rr}, device_id_type=mesh_id)
            return c

        lax.fori_loop(1, n, greet, 0)
        pl.semaphore_signal(bar, device_id=partner, device_id_type=mesh_id)

        def qcopy(h, c):
            local(q_hbm.at[:, pl.ds(pl.multiple_of(h * HW, HW), HW)], q_s.at[h], lsem.at[0]).start()
            return c

        lax.fori_loop(0, heads, qcopy, 0)
        local(ids_hbm, ids_s, lsem.at[4]).start()
        local(rw_hbm, rw_s, lsem.at[5]).start()
        local(len_hbm, len_s, lsem.at[1]).start()
        local(tk_hbm, tk_s, lsem.at[2]).start()
        local(tv_hbm, tv_s, lsem.at[3]).start()
        local(k_hbm, k_s, lsem.at[6]).start()
        local(v_hbm, v_s, lsem.at[7]).start()
        local(ow_hbm.at[:, columns(r, v)], wb.at[v, r], lsem.at[9]).start()
        local(res_hbm.at[:, columns(r, v)], res.at[v, r], lsem.at[10]).start()
        local(gain_hbm, gain_s, lsem.at[8]).start()
        units = wg_hbm.shape[2]
        first_units, last_units = pl.ds(0, units), pl.ds(units, units)
        local(wg_hbm.at[0], wgu.at[:, first_units], lsem.at[11]).start()
        local(wu_hbm.at[0], wgu.at[:, last_units], lsem.at[12]).start()
        local(wd_hbm.at[0, :, pl.ds(pl.multiple_of(r * half, half), half)], wdn.at[first_units], lsem.at[13]).start()

    with scope("ids"):
        local(ids_hbm, ids_s, lsem.at[4]).wait()
        local(rw_hbm, rw_s, lsem.at[5]).wait()
        weight = rw_s[...]
        mixing = weight / jnp.sum(weight, axis=1, keepdims=True)
        lane = iota((tok, HW), 1)
        row = iota((tok, HW), 0)
        place = (lane == v * tok + row).astype(F32)
        place_mix = (lane == tokens + v * tok + row).astype(F32)
        exact = lax.Precision.HIGHEST
        idt[...] = dot(ids_s[...].astype(F32), place, ((0,), (0,)), exact) + dot(mixing, place_mix, ((0,), (0,)), exact)
        id1[v] = idt[...]
    with scope("barrier_wait"):
        pl.semaphore_wait(bar, 4 * (n - 1) + 1)

    with scope("weights_send"):

        def wsend(d, c):
            vv, uu = around(v, d), around(u, d)
            remote(idt, id1.at[v], 5, id1sem, own(u, vv)).start()
            remote(ow_hbm.at[:, columns(r, vv)], wb.at[v, r], 0, wsem.at[0], own(u, vv)).start()
            remote(ow_hbm.at[:, columns(1 - r, uu)], wb.at[u, r], 1, wsem.at[1], across(uu, v)).start()

        each(wsend)
        remote(ow_hbm.at[:, columns(1 - r, u)], wb.at[u, r], 1, wsem.at[1], partner).start()

    with scope("attention"):
        kvh = k_s.shape[2] // HW
        per = heads // kvh
        rows = per * seqs
        arrived(q_s, lsem.at[0])
        local(len_hbm, len_s, lsem.at[1]).wait()
        local(tk_hbm, tk_s, lsem.at[2]).wait()
        local(tv_hbm, tv_s, lsem.at[3]).wait()
        local(k_hbm, k_s, lsem.at[6]).wait()
        inv_root = 1.0 / math.sqrt(HW)
        rowseq = lax.rem(iota((rows, pos), 0), seqs)
        colpos = iota((rows, pos), 1)
        visible = jnp.concatenate(
            [jnp.where((rowseq == s) & (colpos < len_s[s]), 0.0, NEG) for s in range(seqs)], axis=1
        )
        fresh_ok = lax.rem(iota((rows, seqs), 0), seqs) == iota((rows, seqs), 1)
        for g in range(kvh):
            at = slice(g * HW, (g + 1) * HW)
            qg = q_s[g * per : (g + 1) * per].reshape(rows, HW)
            kg = k_s[:, :, at].reshape(seqs * pos, HW)
            s_old = dot(qg, kg, ((1,), (1,))) * inv_root + visible
            s_new = jnp.where(fresh_ok, dot(qg, tk_s[:, at], ((1,), (1,))) * inv_root, NEG)
            top = jnp.maximum(jnp.max(s_old, axis=1, keepdims=True), jnp.max(s_new, axis=1, keepdims=True))
            p_old = jnp.exp(s_old - top)
            p_new = jnp.exp(s_new - top)
            scale = 1.0 / (jnp.sum(p_old, axis=1, keepdims=True) + jnp.sum(p_new, axis=1, keepdims=True))
            p_old = (p_old * scale).astype(BF)
            p_new = (p_new * scale).astype(BF).astype(F32)
            if g == 0:
                local(v_hbm, v_s, lsem.at[7]).wait()
            vg = v_s[:, :, at].reshape(seqs * pos, HW)
            mixed = dot(p_old, vg)
            tv = tv_s[:, at].astype(F32)
            for s in range(seqs):
                mixed = mixed + p_new[:, s : s + 1] * tv[s : s + 1, :]
            att[g * (n // kvh) : (g + 1) * (n // kvh)] = mixed.astype(BF).reshape(n // kvh, n, seqs, HW)

    with scope("feature_send"):
        mine = pl.ds(r * seqs, seqs)

        def t1send(d, c):
            xx, yy = around(x, d), around(y, d)
            ahead = d // (n // 2)
            place = ahead * (2 * (n - d) - 1) + (1 - ahead) * 2 * d
            rows_at = pl.ds(place * tok + r * seqs, seqs)
            remote(att.at[xx], xs.at[y, :, rows_at], 7, t1sem.at[place], {"expert": xx * n + y, "replica": 0}).start()
            remote(att.at[:, yy], xs.at[x, :, rows_at], 7, t1sem.at[place], {"expert": x * n + yy, "replica": 1}).start()

        each(t1send)

        @pl.when(r == 0)
        def _():
            remote(att.at[:, y], xs.at[x, :, mine], 7, t1sem.at[0], partner).start()
            local(att.at[x], xs.at[y, :, mine], lsem.at[14]).start()

        @pl.when(r == 1)
        def _():
            remote(att.at[x], xs.at[y, :, mine], 7, t1sem.at[0], partner).start()
            local(att.at[:, y], xs.at[x, :, mine], lsem.at[14]).start()

        arrived(att.at[0], lsem.at[14])

        def rsend(d, c):
            vv, uu = around(v, d), around(u, d)
            remote(res_hbm.at[:, columns(r, vv)], res.at[v, r], 2, rsem.at[0], own(u, vv)).start()
            remote(res_hbm.at[:, columns(1 - r, uu)], res.at[u, r], 3, rsem.at[1], across(uu, v)).start()

        each(rsend)
        remote(res_hbm.at[:, columns(1 - r, u)], res.at[u, r], 3, rsem.at[1], partner).start()
        remote(wd_hbm.at[0, :, pl.ds(pl.multiple_of((1 - r) * half, half), half)], wdn.at[last_units], 4, dsem.at[0], partner).start()

    chunks = n // 2
    crows = tokens // chunks

    def chunk_of(w, c):
        return xs.at[w, :, pl.ds(c * crows, crows)]

    def pass_on(w, c, d):
        remote(chunk_of(w, c), chunk_of(w, c), 8, xsem.at[w, c], own(u, around(v, d))).start()

    def start_chunk(c):
        for place in (2 * c, 2 * c + 1):
            if place == 0:
                arrived(att.at[0], t1sem.at[0])
            else:
                arrived(att.at[pl.ds(0, 2)], t1sem.at[place])
        pass_on(v, c, 1)
        pass_on(v, c, n - 1)

    def relay(s, c):
        behind, ahead = around(v, n - s), around(v, s)
        arrived(chunk_of(behind, c), xsem.at[behind, c])
        if s < n // 2 - 1 or c % 2 == 0:
            pass_on(behind, c, 1)
        arrived(chunk_of(ahead, c), xsem.at[ahead, c])
        if s < n // 2 - 1 or c % 2 == 1:
            pass_on(ahead, c, n - 1)

    wv = wb.reshape(n * HW, cols)

    def project(blocks):
        lhs = jnp.concatenate(
            [jnp.concatenate([xs[w, k] for k in range(n)], axis=1) for w in blocks], axis=0
        )
        part = dot(lhs, wv[...]).astype(BF)
        for i, w in enumerate(blocks):
            ysend[:, w] = part[i * tokens : (i + 1) * tokens].reshape(n, tok, cols)
            rbuf[u, w] = ysend[0, w]

        def to(d, c):
            uu = around(u, d)
            ahead = d // (n // 2 + 1)
            place = (1 - ahead) * (2 * d - 1) + ahead * 2 * (n - d)
            for w in blocks:
                remote(ysend.at[place, w], rbuf.at[u, w], 9, rrsem, own(uu, v)).start()

        each(to)

    with scope("gather_start"):
        start_chunk(0)
        start_chunk(1)
        start_chunk(2)
        relay(1, 0)
        start_chunk(3)
        relay(1, 1)
        relay(1, 2)
        relay(1, 3)
    with scope("weights_wait"):
        local(ow_hbm.at[:, columns(r, v)], wb.at[v, r], lsem.at[9]).wait()
        arrived(wb.at[most, 0], wsem.at[0])
        arrived(wb.at[:, 0], wsem.at[1])
    with scope("project0"):
        project([v])
    with scope("relay2"):
        for c in range(chunks):
            relay(2, c)
    with scope("project1"):
        project([around(v, 1), around(v, n - 1)])
    with scope("relay3"):
        for c in range(chunks):
            relay(3, c)
    with scope("project2"):
        project([around(v, 2), around(v, n - 2)])
    with scope("ids_second"):
        arrived(id1.at[most], id1sem)
        idg[...] = functools.reduce(lambda p, q: p + q, [id1[i] for i in range(n)])

        def id2send(d, c):
            remote(idg, id2.at[u], 6, id2sem, own(around(u, d), v)).start()

        each(id2send)
        id2[u] = idg[...]
    with scope("project3"):
        project([around(v, 3), around(v, n - 3)])
    with scope("relay4"):
        opposite = around(v, n // 2)
        for c in range(chunks):
            arrived(chunk_of(opposite, c), xsem.at[opposite, c])
    with scope("project4"):
        project([opposite])

    with scope("tables_wait"):
        arrived(id2.at[most], id2sem)
    with scope("tables"):
        block = (iota((n, HW), 1) // tok == iota((n, HW), 0)).astype(F32)
        before = (
            (iota((HW, HW), 0) // tok == iota((HW, HW), 1) // tok) & (iota((HW, HW), 0) < iota((HW, HW), 1))
        ).astype(BF)
        place_v = iota((n, 1), 0).astype(F32)
        ue = u.astype(F32)
        ve = v.astype(F32)
        ae = a.astype(F32)
        be = b.astype(F32)
        expert_v = ae * ue + be * place_v
        named = []
        for i in range(n):
            got = id2[i]
            named.append(functools.reduce(lambda p, q: p + q, [(got[k : k + 1] == expert_v).astype(F32) for k in range(topk)]))
        named = jnp.concatenate(named, axis=0)
        rank = dot(named.astype(BF), before)
        for i in range(n):
            here = slice(i * n, (i + 1) * n)
            picks = []
            for j in range(SLOTS):
                hit = jnp.where(rank[here] == j, named[here], 0.0)
                picks.append(hit[:, None, :] * block[None])
            pbuf[i] = jnp.stack(picks, axis=1).reshape(HW, HW).astype(BF)
        got = idg[...]
        back = pltpu.roll(got, tokens, 1)
        expert_u = ae * place_v + be * ve
        same = [got[k : k + 1] == expert_u for k in range(topk)]
        chosen = functools.reduce(lambda p, q: p + q, [s.astype(F32) for s in same])
        mix = functools.reduce(lambda p, q: p + q, [jnp.where(s, back[k : k + 1], 0.0) for k, s in enumerate(same)])
        rank = dot(jnp.concatenate([chosen, chosen], axis=0).astype(BF), before)[:n]
        picks = []
        for j in range(SLOTS):
            hit = jnp.where(rank == j, mix, 0.0)
            picks.append(hit[:, None, :] * block[None])
        table = jnp.stack(picks, axis=1).reshape(HW, HW)
        high = table.astype(BF)
        low = (table - high.astype(F32)).astype(BF)
        ctb[...] = jnp.concatenate([high[:, :tokens], low[:, :tokens]], axis=1)

    with scope("residual_wait"):
        local(res_hbm.at[:, columns(r, v)], res.at[v, r], lsem.at[10]).wait()
        arrived(res.at[most, 0], rsem.at[0])
        arrived(res.at[:, 0], rsem.at[1])
        local(gain_hbm, gain_s, lsem.at[8]).wait()
        gain = gain_s[columns(r, v)].astype(F32).reshape(1, cols)
    with scope("reduce_wait"):
        arrived(rbuf.at[most], rrsem)
    with scope("hidden"):
        total = res[...].astype(F32).reshape(tokens, cols)
        for i in range(n):
            total = total + rbuf[i].astype(F32).reshape(tokens, cols)
        hg[...] = (total * gain).astype(BF)
        hall[u] = hg[...]

        def d1send(i, c):
            d = far(n - i)
            uu = around(u, d)
            remote(hg, hall.at[u], 10, hsem.at[u], own(uu, v)).start()
            return c

        lax.fori_loop(1, n, d1send, 0)
        hid[...] = total.reshape(n, tok, cols)
        square = (total * total).astype(BF)
        sums = dot(jnp.ones((n, cols), BF), square, ((1,), (1,)))
        ss0[...] = jnp.concatenate([sums, jnp.zeros((n, HW - tokens), F32)], axis=1)
        ss1[v] = ss0[...]

        def ss1send(d, c):
            remote(ss0, ss1.at[v], 11, ss1sem, own(u, around(v, d))).start()

        each(ss1send)

    def pack(groups):
        for uu in groups:
            tsend[uu] = dot(pbuf[uu, :, pl.ds(0, tokens)], hall[uu]).astype(BF).reshape(n, slots, cols)

        def to(d, c):
            vv = around(v, d)
            for uu in groups:
                remote(tsend.at[uu, vv], town.at[v, uu], 13, tsem.at[uu], own(u, vv)).start()

        each(to)
        for uu in groups:
            town[v, uu] = tsend[uu, v]

    def pair(s):
        if s == 0:
            return [u]
        if 2 * s == n:
            return [around(u, s)]
        return [around(u, s), around(u, n - s)]

    def pack_pair(s):
        for uu in pair(s):
            if s > 0:
                arrived(hall.at[uu], hsem.at[uu])
        pack(pair(s))

    def hand_over(s):
        for uu in pair(s):
            arrived(town.at[most, uu], tsem.at[uu])
            remote(town.at[:, uu], toth.at[:, uu], 15, osem.at[uu], partner).start()

    with scope("pack0"):
        pack_pair(0)
    with scope("pack1"):
        pack_pair(1)

        def hmsend(d, c):
            vv = around(v, d)
            remote(hid.at[vv, mine], hm.at[0, v], 12, hmsem.at[0], own(u, vv)).start()
            remote(hid.at[vv, pl.ds((1 - r) * seqs, seqs)], hm.at[1, v], 16, hmsem.at[1], across(u, vv)).start()

        each(hmsend)
        remote(hid.at[v, pl.ds((1 - r) * seqs, seqs)], hm.at[1, v], 16, hmsem.at[1], partner).start()
        local(hid.at[v, mine], hm.at[0, v], lsem.at[1]).start()
        arrived(hm.at[0, 0], lsem.at[1])
    with scope("pack2"):
        pack_pair(2)
    with scope("pack3"):
        pack_pair(3)
    with scope("sums_second"):
        arrived(ss1.at[most], ss1sem)
        ss2t[...] = functools.reduce(lambda p, q: p + q, [ss1[i] for i in range(n)])

        def ss2send(d, c):
            remote(ss2t, ss2.at[u], 14, ss2sem, own(around(u, d), v)).start()

        each(ss2send)
        ss2[u] = ss2t[...]
    with scope("pack4"):
        pack_pair(4)
    with scope("hand0"):
        hand_over(0)
        hand_over(1)
        hand_over(2)
    with scope("expert_weights"):
        local(wg_hbm.at[0], wgu.at[:, first_units], lsem.at[11]).wait()
        local(wu_hbm.at[0], wgu.at[:, last_units], lsem.at[12]).wait()
    with scope("hand3"):
        hand_over(3)
    with scope("hand4"):
        hand_over(4)
    with scope("sums_third"):
        arrived(ss2.at[most], ss2sem)
        for i in range(n):
            part = pbuf[i, pl.ds(pl.multiple_of(v * slots, slots), slots), :].astype(F32)
            column = jnp.sum(part * ss2[i][0:1], axis=1, keepdims=True)
            sso[i * slots : (i + 1) * slots, :] = jnp.broadcast_to(column, (slots, HW))
        remote(sso, ssp, 17, dsem.at[1], partner).start()
    with scope("gate_up_own"):
        tiles = accx.shape[0]
        tv_own = town.reshape(n, HW, cols)
        tv_oth = toth.reshape(n, HW, cols)

        def product(ref, plane):
            lhs = jnp.concatenate([ref[i] for i in range(n)], axis=1)
            return dot(lhs, wgu[pl.ds(pl.multiple_of(plane * half, half), half), :])

        acco[...] = product(tv_own, r)
    with scope("gate_up_other"):
        for i in range(n):
            arrived(toth.at[:, i], osem.at[i])
        part = product(tv_oth, 1 - r)
        for t in range(tiles):
            accx[t] = part[:, t * HW : (t + 1) * HW]

    with scope("activation"):
        arrived(ssp, dsem.at[1])

        def swapped(ref):
            return jnp.concatenate(
                [ref[pl.ds(j * n + i, n, stride=slots), :] for i in range(n) for j in range(SLOTS)], axis=0
            )

        model = 2 * half
        scale = lax.rsqrt((sso[...] + swapped(ssp)) * (1.0 / model) + 1e-06)
        up_at = tiles // 2
        for t in range(up_at):
            gate = (acco[:, t * HW : (t + 1) * HW] + swapped(accx.at[t])) * scale
            up = (acco[:, (t + up_at) * HW : (t + up_at + 1) * HW] + swapped(accx.at[t + up_at])) * scale
            act = gate / (1.0 + jnp.exp(-gate)) * up
            acto[:, t * HW : (t + 1) * HW] = act.astype(BF)
            scr[t] = act
        for t in range(up_at):
            acts[:, t * HW : (t + 1) * HW] = swapped(scr.at[t]).astype(BF)
        remote(acts, actx, 18, dsem.at[2], partner).start()
    with scope("activation_wait"):
        local(wd_hbm.at[0, :, pl.ds(0, half)], wdn.at[first_units], lsem.at[13]).wait()
        arrived(wdn.at[last_units], dsem.at[0])
        arrived(actx, dsem.at[2])

    with scope("down"):
        ov = osend.reshape(n, HW, cols)

        def down(i, c):
            at = pl.ds(pl.multiple_of(i * cols, cols), cols)
            lhs = jnp.concatenate([acto[...], actx[...]], axis=1)
            ov[i] = dot(lhs, wdn[:, at]).astype(BF)

            def to(d, cc):
                uu = around(u, d)
                remote(osend.at[i, uu], gbuf.at[i, u], 19, gsem.at[i], own(uu, v)).start()

            each(to)
            gbuf[i, u] = osend[i, u]
            return c

        lax.fori_loop(0, n, down, 0)

    with scope("combine"):
        gv = gbuf.reshape(n, HW, cols)

        def combine(i, c):
            arrived(gbuf.at[i, most], gsem.at[i])
            both = dot(ctb[...], gv[i], ((0,), (0,)))
            csend[i] = (both[:tokens] + both[tokens:]).astype(BF).reshape(n, tok, cols)

            def to(d, cc):
                vv = around(v, d)
                remote(csend.at[i, vv, mine], zbuf.at[i, 0, v], 20, zsem.at[i, 0], own(u, vv)).start()
                remote(csend.at[i, vv, pl.ds((1 - r) * seqs, seqs)], zbuf.at[i, 1, v], 21, zsem.at[i, 1], across(u, vv)).start()

            each(to)
            remote(csend.at[i, v, pl.ds((1 - r) * seqs, seqs)], zbuf.at[i, 1, v], 21, zsem.at[i, 1], partner).start()
            local(csend.at[i, v, mine], zbuf.at[i, 0, v], lsem.at[0]).start()
            arrived(zbuf.at[0, 0, 0], lsem.at[0])
            return c

        lax.fori_loop(0, n, combine, 0)
    with scope("home_wait"):
        arrived(hm.at[0, most], hmsem.at[0])
        arrived(hm.at[1], hmsem.at[1])
    with scope("final"):
        def final(i, c):
            arrived(zbuf.at[i, 0, most], zsem.at[i, 0])
            arrived(zbuf.at[i, 1], zsem.at[i, 1])
            for p in (0, 1):
                total = hm[p, i]
                for j in range(n):
                    total = total + zbuf[i, p, j].astype(F32)
                plane = r + p - 2 * r * p
                out_ref[:, columns(plane, i)] = total.astype(BF)
            return c

        lax.fori_loop(0, n, final, 0)

    with scope("drain"):
        for send, ref in enumerate((
            wb.at[most, 0], wb.at[:, 0], res.at[most, 0], res.at[:, 0], wdn.at[last_units], id1.at[most], id2.at[most],
            xs.at[0, :, pl.ds(0, (2 * n - 1) * seqs)], xs.at[most], rbuf.at[most], hall.at[most], ss1.at[most], hm.at[0, most],
            town.at[most], ss2.at[most], town, hm.at[1], sso, acts, gbuf.at[most], zbuf.at[:, 0, most], zbuf.at[:, 1],
        )):
            arrived(ref, ssem.at[send])


def solution(mesh):
    n = math.isqrt(mesh.shape["expert"])

    def on_device(queries, token_keys, token_values, stored_keys, stored_values, kv_len, residual, out_weight, norm_gain,
                  expert_ids, route_weight, w_gate, w_up, w_down):
        seqs, pos, kvw = stored_keys.shape
        heads = queries.shape[1] // HW
        model = residual.shape[1]
        half = model // 2
        cols = half // n
        tok, topk = expert_ids.shape
        hidden = w_gate.shape[2]
        tokens = n * tok
        slots = SLOTS * n
        tiles = 2 * hidden // HW
        wrows = out_weight.shape[0]
        vmem = pltpu.VMEM
        dma = pltpu.SemaphoreType.DMA
        scratch = [
            vmem((heads, seqs, HW), BF), vmem((seqs, kvw), BF), vmem((seqs, kvw), BF),
            vmem((seqs, pos, kvw), BF), vmem((seqs, pos, kvw), BF), pltpu.SMEM((seqs,), jnp.int32),
            vmem((model,), BF), vmem((tok, topk), jnp.int32), vmem((tok, topk), F32),
            vmem((model, 2 * hidden), BF), vmem((2 * hidden, half), BF),
            vmem((n, 2, wrows, cols), BF), vmem((n, 2, seqs, cols), BF),
            vmem((n, n, seqs, HW), BF), vmem((n, n, tokens, HW), BF),
            vmem((n, n, tok, cols), BF), vmem((n, n, tok, cols), BF),
            vmem((n, tok, cols), F32), vmem((tokens, cols), BF), vmem((2, n, seqs, cols), F32),
            vmem((n, tokens, cols), BF), vmem((n, n, slots, cols), BF), vmem((n, n, slots, cols), BF), vmem((n, n, slots, cols), BF),
            vmem((topk, HW), F32), vmem((n, topk, HW), F32), vmem((topk, HW), F32), vmem((n, topk, HW), F32),
            vmem((n, HW, HW), BF), vmem((HW, 2 * tokens), BF),
            vmem((n, HW), F32), vmem((n, n, HW), F32), vmem((n, HW), F32), vmem((n, n, HW), F32),
            vmem((HW, HW), F32), vmem((HW, HW), F32),
            vmem((HW, 2 * hidden), F32), vmem((tiles, HW, HW), F32), vmem((tiles // 2, HW, HW), F32),
            vmem((HW, hidden), BF), vmem((HW, hidden), BF), vmem((HW, hidden), BF),
            vmem((n, n, slots, cols), BF), vmem((n, n, slots, cols), BF),
            vmem((n, n, tok, cols), BF), vmem((n, 2, n, seqs, cols), BF),
            dma((15,)), dma((22,)), dma((2,)), dma((2,)), dma((n,)), dma((n, n // 2)), dma, dma((2,)), dma((n,)), dma((n,)), dma((n,)),
            dma, dma, dma, dma, dma((3,)), dma((n,)), dma((n, 2)),
        ]
        return pl.pallas_call(
            functools.partial(kernel, n),
            out_shape=jax.ShapeDtypeStruct(residual.shape, BF),
            in_specs=[pl.BlockSpec(memory_space=pl.ANY)] * 14,
            out_specs=pl.BlockSpec(memory_space=pltpu.VMEM),
            scratch_shapes=scratch,
            compiler_params=pltpu.CompilerParams(
                collective_id=0, has_side_effects=True, vmem_limit_bytes=60 * 1024 * 1024
            ),
        )(queries, token_keys, token_values, stored_keys, stored_values, kv_len, residual, out_weight, norm_gain,
          expert_ids, route_weight, w_gate, w_up, w_down)

    everyone = ("groups", "expert", "replica")
    in_specs = (
        P(everyone, None), P(everyone, None), P(everyone, None), P(everyone, None, None), P(everyone, None, None),
        P(everyone), P(everyone, None), P(("expert", "replica"), None), P(), P(("groups", "expert"), None),
        P(("groups", "expert"), None), P("expert", None, "replica"), P("expert", None, "replica"), P("expert", "replica", None),
    )
    return jax.shard_map(
        on_device, mesh=mesh, in_specs=in_specs, out_specs=P(everyone, None), check_vma=False
    )
```

time: 101 us -> 91.9 us (0.910)
  Pallas kernels: 99.9 us -> 90.3 us
    pallas_call x1, Pallas kernels: 99.9 us -> 90.3 us  [on_device(): pl.pallas_call(functools.partial(kernel, n), out_shape=jax.ShapeDtypeStru...]
where the time goes in v2:
time: 91.9 us; the launch traced here: 91.7 us
  Pallas kernels  90.3 us (98%)
  local copies, waits for them, and re-layouts  1.39 us (2%)
    pallas_call x1, Pallas kernels, on_device(): pl.pallas_call(functools.partial(kernel, n), out_shape=jax.ShapeDtypeStru...  90.3 us

profile of v2, /device:TPU:513, one launch (start us, length us, event | category | flops | bytes accessed | tf_op | source)
XLA Modules:
  0.0 91.7 jit_solution(11629862899897736619)
XLA Ops:
  0.0 90.3 %shard_map.136 = bf16[4,4096]{1,0:T(4,128)(2,1)} custom-call(bf16[4,8192]{1,0:T(4,128)(2,1)} %q_hbm.1, bf16[4,512]{1,0:T(4,128)(2,1)} %tk_hbm.1, bf16[4,512]{1,0:T(4,128)(2,1)} %tv_hbm.1, bf16[4,256,512]{2,1,0:T(8,128)(2,1)} %k_hbm.1, bf16[4,256,512]{2,1,0:T(8,128)(2,1)} %v_hbm.1, s32[4]{0:T(128)} %len_hbm.1, bf16[4,4096]{1,0:T(4,128)(2,1)} %res_hbm.1, ...), custom_call_target="tpu_custom_call" | custom-call | tf_op jit(solution)/shard_map/pallas_call | solution.py:603
  90.3 1.4 %copy.16 = bf16[4,4096]{1,0:T(4,128)(2,1)} copy(bf16[4,4096]{1,0:T(4,128)(2,1)} %shard_map.136) | data formatting | bytes 65536

commit v3 on v2

--- a/solution.py
+++ b/solution.py
@@ -27,10 +27,10 @@
     n, q_hbm, tk_hbm, tv_hbm, k_hbm, v_hbm, len_hbm, res_hbm, ow_hbm, gain_hbm, ids_hbm, rw_hbm, wg_hbm, wu_hbm, wd_hbm,
     out_ref,
     q_s, tk_s, tv_s, k_s, v_s, len_s, gain_s, ids_s, rw_s, wgu, wdn,
-    wb, res, att, xs, ysend, rbuf, hid, hg, hm, hall, tsend, town, toth,
+    wb, wst, res, att, xs, ysend, rbuf, hid, hg, hm, hall, tsend, town, toth,
     idt, id1, idg, id2, pbuf, ctb, ss0, ss1, ss2t, ss2, sso, ssp,
     acco, accx, scr, acto, acts, actx, osend, gbuf, csend, zbuf,
-    lsem, ssem, wsem, rsem, t1sem, xsem, rrsem, hmsem, hsem, tsem, osem, ss1sem, ss2sem, id1sem, id2sem, dsem, gsem, zsem,
+    lsem, ssem, wsem, rsem, t1sem, xsem, rrsem, hmsem, hsem, tsem, osem, ss1sem, ss2sem, id1sem, id2sem, dsem, gsem, zsem, ready,
 ):
     r = lax.axis_index("replica")
     e = lax.axis_index("expert")
@@ -82,64 +82,72 @@
 
     scope = jax.named_scope
 
-    with scope("barrier"):
-        bar = pltpu.get_barrier_semaphore()
-
-        def greet(d, c):
-            for rr in (0, 1):
-                pl.semaphore_signal(bar, device_id={"expert": around(x, d) * n + y, "replica": rr}, device_id_type=mesh_id)
-                pl.semaphore_signal(bar, device_id={"expert": x * n + around(y, d), "replica": rr}, device_id_type=mesh_id)
-            return c
-
-        lax.fori_loop(1, n, greet, 0)
-        pl.semaphore_signal(bar, device_id=partner, device_id_type=mesh_id)
+    units = wg_hbm.shape[2]
+    first_units, last_units = pl.ds(0, units), pl.ds(units, units)
+    with scope("loads"):
+        local(k_hbm, k_s, lsem.at[6]).start()
 
         def qcopy(h, c):
             local(q_hbm.at[:, pl.ds(pl.multiple_of(h * HW, HW), HW)], q_s.at[h], lsem.at[0]).start()
             return c
 
         lax.fori_loop(0, heads, qcopy, 0)
-        local(ids_hbm, ids_s, lsem.at[4]).start()
-        local(rw_hbm, rw_s, lsem.at[5]).start()
         local(len_hbm, len_s, lsem.at[1]).start()
         local(tk_hbm, tk_s, lsem.at[2]).start()
         local(tv_hbm, tv_s, lsem.at[3]).start()
-        local(k_hbm, k_s, lsem.at[6]).start()
         local(v_hbm, v_s, lsem.at[7]).start()
-        local(ow_hbm.at[:, columns(r, v)], wb.at[v, r], lsem.at[9]).start()
+        local(ids_hbm, ids_s, lsem.at[4]).start()
+        local(rw_hbm, rw_s, lsem.at[5]).start()
+
+    with scope("barrier"):
+        bar = pltpu.get_barrier_semaphore()
+
+        def peers(sem):
+            def to(d, c):
+                pl.semaphore_signal(sem, device_id={"expert": around(x, d) * n + y, "replica": 1}, device_id_type=mesh_id)
+                pl.semaphore_signal(sem, device_id={"expert": x * n + around(y, d), "replica": 1}, device_id_type=mesh_id)
+                return c
+
+            lax.fori_loop(1, n, to, 0)
+
+        @pl.when(r == 1)
+        def _():
+            peers(bar)
+
+        pl.semaphore_wait(bar, r * 2 * (n - 1) + (1 - r))
+
+        @pl.when(r == 1)
+        def _():
+            pl.semaphore_signal(bar, device_id=partner, device_id_type=mesh_id)
+
+        @pl.when(r == 0)
+        def _():
+            pl.semaphore_signal(ready.at[0], device_id=partner, device_id_type=mesh_id)
+
+    with scope("weights_send"):
+
+        def wsend(d, c):
+            xx, yy = around(x, d), around(y, d)
+            remote(ow_hbm.at[:, columns(0, yy)], wst.at[y, r], 0, wsem.at[0, r], {"expert": x * n + yy, "replica": 1}).start()
+            remote(ow_hbm.at[:, columns(1, xx)], wb.at[x, r], 1, wsem.at[1, r], {"expert": xx * n + y, "replica": 1}).start()
+
+        each(wsend)
+
+        @pl.when(r == 1)
+        def _():
+            local(ow_hbm.at[:, columns(0, y)], wst.at[y, r], lsem.at[9]).start()
+            local(ow_hbm.at[:, columns(1, x)], wb.at[x, r], lsem.at[9]).start()
+
+        @pl.when(r == 0)
+        def _():
+            remote(ow_hbm.at[:, columns(0, y)], wst.at[y, r], 2, wsem.at[0, 2], partner).start()
+            remote(ow_hbm.at[:, columns(1, x)], wb.at[x, r], 3, wsem.at[1, 2], partner).start()
+
         local(res_hbm.at[:, columns(r, v)], res.at[v, r], lsem.at[10]).start()
         local(gain_hbm, gain_s, lsem.at[8]).start()
-        units = wg_hbm.shape[2]
-        first_units, last_units = pl.ds(0, units), pl.ds(units, units)
         local(wg_hbm.at[0], wgu.at[:, first_units], lsem.at[11]).start()
         local(wu_hbm.at[0], wgu.at[:, last_units], lsem.at[12]).start()
         local(wd_hbm.at[0, :, pl.ds(pl.multiple_of(r * half, half), half)], wdn.at[first_units], lsem.at[13]).start()
-
-    with scope("ids"):
-        local(ids_hbm, ids_s, lsem.at[4]).wait()
-        local(rw_hbm, rw_s, lsem.at[5]).wait()
-        weight = rw_s[...]
-        mixing = weight / jnp.sum(weight, axis=1, keepdims=True)
-        lane = iota((tok, HW), 1)
-        row = iota((tok, HW), 0)
-        place = (lane == v * tok + row).astype(F32)
-        place_mix = (lane == tokens + v * tok + row).astype(F32)
-        exact = lax.Precision.HIGHEST
-        idt[...] = dot(ids_s[...].astype(F32), place, ((0,), (0,)), exact) + dot(mixing, place_mix, ((0,), (0,)), exact)
-        id1[v] = idt[...]
-    with scope("barrier_wait"):
-        pl.semaphore_wait(bar, 4 * (n - 1) + 1)
-
-    with scope("weights_send"):
-
-        def wsend(d, c):
-            vv, uu = around(v, d), around(u, d)
-            remote(idt, id1.at[v], 5, id1sem, own(u, vv)).start()
-            remote(ow_hbm.at[:, columns(r, vv)], wb.at[v, r], 0, wsem.at[0], own(u, vv)).start()
-            remote(ow_hbm.at[:, columns(1 - r, uu)], wb.at[u, r], 1, wsem.at[1], across(uu, v)).start()
-
-        each(wsend)
-        remote(ow_hbm.at[:, columns(1 - r, u)], wb.at[u, r], 1, wsem.at[1], partner).start()
 
     with scope("attention"):
         kvh = k_s.shape[2] // HW
@@ -178,8 +186,42 @@
                 mixed = mixed + p_new[:, s : s + 1] * tv[s : s + 1, :]
             att[g * (n // kvh) : (g + 1) * (n // kvh)] = mixed.astype(BF).reshape(n // kvh, n, seqs, HW)
 
+    with scope("ids"):
+        local(ids_hbm, ids_s, lsem.at[4]).wait()
+        local(rw_hbm, rw_s, lsem.at[5]).wait()
+        weight = rw_s[...]
+        mixing = weight / jnp.sum(weight, axis=1, keepdims=True)
+        lane = iota((tok, HW), 1)
+        row = iota((tok, HW), 0)
+        place = (lane == v * tok + row).astype(F32)
+        place_mix = (lane == tokens + v * tok + row).astype(F32)
+        exact = lax.Precision.HIGHEST
+        idt[...] = dot(ids_s[...].astype(F32), place, ((0,), (0,)), exact) + dot(mixing, place_mix, ((0,), (0,)), exact)
+        id1[v] = idt[...]
+
+    with scope("barrier_second"):
+
+        @pl.when(r == 1)
+        def _():
+            pl.semaphore_wait(ready.at[0], 1)
+            peers(ready.at[1])
+            pl.semaphore_wait(ready.at[1], 2 * (n - 1))
+            pl.semaphore_signal(ready.at[2], device_id=partner, device_id_type=mesh_id)
+
+        @pl.when(r == 0)
+        def _():
+            pl.semaphore_wait(ready.at[2], 1)
+
     with scope("feature_send"):
         mine = pl.ds(r * seqs, seqs)
+
+        @pl.when(r == 0)
+        def _():
+            remote(att.at[:, y], xs.at[x, :, mine], 7, t1sem.at[0], partner).start()
+
+        @pl.when(r == 1)
+        def _():
+            remote(att.at[x], xs.at[y, :, mine], 7, t1sem.at[0], partner).start()
 
         def t1send(d, c):
             xx, yy = around(x, d), around(y, d)
@@ -193,23 +235,28 @@
 
         @pl.when(r == 0)
         def _():
-            remote(att.at[:, y], xs.at[x, :, mine], 7, t1sem.at[0], partner).start()
             local(att.at[x], xs.at[y, :, mine], lsem.at[14]).start()
 
         @pl.when(r == 1)
         def _():
-            remote(att.at[x], xs.at[y, :, mine], 7, t1sem.at[0], partner).start()
             local(att.at[:, y], xs.at[x, :, mine], lsem.at[14]).start()
 
         arrived(att.at[0], lsem.at[14])
+
+    with scope("small_send"):
+
+        def idsend(d, c):
+            remote(idt, id1.at[v], 5, id1sem, own(u, around(v, d))).start()
+
+        each(idsend)
 
         def rsend(d, c):
             vv, uu = around(v, d), around(u, d)
-            remote(res_hbm.at[:, columns(r, vv)], res.at[v, r], 2, rsem.at[0], own(u, vv)).start()
-            remote(res_hbm.at[:, columns(1 - r, uu)], res.at[u, r], 3, rsem.at[1], across(uu, v)).start()
+            remote(res_hbm.at[:, columns(r, vv)], res.at[v, r], 22, rsem.at[0], own(u, vv)).start()
+            remote(res_hbm.at[:, columns(1 - r, uu)], res.at[u, r], 23, rsem.at[1], across(uu, v)).start()
 
         each(rsend)
-        remote(res_hbm.at[:, columns(1 - r, u)], res.at[u, r], 3, rsem.at[1], partner).start()
+        remote(res_hbm.at[:, columns(1 - r, u)], res.at[u, r], 23, rsem.at[1], partner).start()
         remote(wd_hbm.at[0, :, pl.ds(pl.multiple_of((1 - r) * half, half), half)], wdn.at[last_units], 4, dsem.at[0], partner).start()
 
     chunks = n // 2
@@ -227,17 +274,24 @@
                 arrived(att.at[0], t1sem.at[0])
             else:
                 arrived(att.at[pl.ds(0, 2)], t1sem.at[place])
-        pass_on(v, c, 1)
-        pass_on(v, c, n - 1)
-
-    def relay(s, c):
-        behind, ahead = around(v, n - s), around(v, s)
+        for d in (2, n - 2, 1, n - 1):
+            pass_on(v, c, d)
+
+    def relay(c):
+        behind, ahead = around(v, n - 2), around(v, 2)
         arrived(chunk_of(behind, c), xsem.at[behind, c])
-        if s < n // 2 - 1 or c % 2 == 0:
-            pass_on(behind, c, 1)
+        if c % 2 == 0:
+            pass_on(behind, c, 2)
+        pass_on(behind, c, 1)
         arrived(chunk_of(ahead, c), xsem.at[ahead, c])
-        if s < n // 2 - 1 or c % 2 == 1:
-            pass_on(ahead, c, n - 1)
+        if c % 2 == 1:
+            pass_on(ahead, c, n - 2)
+        pass_on(ahead, c, n - 1)
+
+    def gathered(d):
+        w = around(v, d)
+        for c in range(chunks):
+            arrived(chunk_of(w, c), xsem.at[w, c])
 
     wv = wb.reshape(n * HW, cols)
 
@@ -260,30 +314,19 @@
         each(to)
 
     with scope("gather_start"):
-        start_chunk(0)
-        start_chunk(1)
-        start_chunk(2)
-        relay(1, 0)
-        start_chunk(3)
-        relay(1, 1)
-        relay(1, 2)
-        relay(1, 3)
+        for c in range(chunks):
+            start_chunk(c)
     with scope("weights_wait"):
-        local(ow_hbm.at[:, columns(r, v)], wb.at[v, r], lsem.at[9]).wait()
-        arrived(wb.at[most, 0], wsem.at[0])
-        arrived(wb.at[:, 0], wsem.at[1])
-    with scope("project0"):
-        project([v])
-    with scope("relay2"):
-        for c in range(chunks):
-            relay(2, c)
-    with scope("project1"):
-        project([around(v, 1), around(v, n - 1)])
-    with scope("relay3"):
-        for c in range(chunks):
-            relay(3, c)
-    with scope("project2"):
-        project([around(v, 2), around(v, n - 2)])
+
+        @pl.when(r == 1)
+        def _():
+            arrived(wst.at[pl.ds(0, 2), 0], lsem.at[9])
+            for p, buf in enumerate((wst, wb)):
+                arrived(buf.at[most, 0], wsem.at[p, 0])
+                arrived(buf.at[most, 0], wsem.at[p, 1])
+                arrived(buf.at[0, 0], wsem.at[p, 2])
+            remote(wst, wb, 24, dsem.at[3], partner).start()
+
     with scope("ids_second"):
         arrived(id1.at[most], id1sem)
         idg[...] = functools.reduce(lambda p, q: p + q, [id1[i] for i in range(n)])
@@ -293,14 +336,33 @@
 
         each(id2send)
         id2[u] = idg[...]
+    with scope("relay"):
+        for c in range(chunks):
+            relay(c)
+    with scope("weights_wait2"):
+
+        @pl.when(r == 0)
+        def _():
+            arrived(wb, dsem.at[3])
+
+    with scope("project0"):
+        project([v])
+    with scope("gather1"):
+        gathered(1)
+        gathered(n - 1)
+    with scope("project1"):
+        project([around(v, 1), around(v, n - 1)])
+    with scope("project2"):
+        project([around(v, 2), around(v, n - 2)])
+    with scope("gather3"):
+        gathered(3)
+        gathered(n - 3)
     with scope("project3"):
         project([around(v, 3), around(v, n - 3)])
-    with scope("relay4"):
-        opposite = around(v, n // 2)
-        for c in range(chunks):
-            arrived(chunk_of(opposite, c), xsem.at[opposite, c])
+    with scope("gather4"):
+        gathered(n // 2)
     with scope("project4"):
-        project([opposite])
+        project([around(v, n // 2)])
 
     with scope("tables_wait"):
         arrived(id2.at[most], id2sem)
@@ -339,10 +401,10 @@
         for j in range(SLOTS):
             hit = jnp.where(rank == j, mix, 0.0)
             picks.append(hit[:, None, :] * block[None])
-        table = jnp.stack(picks, axis=1).reshape(HW, HW)
-        high = table.astype(BF)
-        low = (table - high.astype(F32)).astype(BF)
-        ctb[...] = jnp.concatenate([high[:, :tokens], low[:, :tokens]], axis=1)
+        table = jnp.transpose(jnp.stack(picks, axis=1).reshape(HW, HW))
+        high = table.astype(BF).astype(F32)
+        low = table - high
+        ctb[...] = jnp.concatenate([high[:tokens], low[:tokens]], axis=0).astype(BF)
 
     with scope("residual_wait"):
         local(res_hbm.at[:, columns(r, v)], res.at[v, r], lsem.at[10]).wait()
@@ -412,16 +474,6 @@
         pack_pair(0)
     with scope("pack1"):
         pack_pair(1)
-
-        def hmsend(d, c):
-            vv = around(v, d)
-            remote(hid.at[vv, mine], hm.at[0, v], 12, hmsem.at[0], own(u, vv)).start()
-            remote(hid.at[vv, pl.ds((1 - r) * seqs, seqs)], hm.at[1, v], 16, hmsem.at[1], across(u, vv)).start()
-
-        each(hmsend)
-        remote(hid.at[v, pl.ds((1 - r) * seqs, seqs)], hm.at[1, v], 16, hmsem.at[1], partner).start()
-        local(hid.at[v, mine], hm.at[0, v], lsem.at[1]).start()
-        arrived(hm.at[0, 0], lsem.at[1])
     with scope("pack2"):
         pack_pair(2)
     with scope("pack3"):
@@ -437,6 +489,17 @@
         ss2[u] = ss2t[...]
     with scope("pack4"):
         pack_pair(4)
+    with scope("hidden_home"):
+
+        def hmsend(d, c):
+            vv = around(v, d)
+            remote(hid.at[vv, mine], hm.at[0, v], 12, hmsem.at[0], own(u, vv)).start()
+            remote(hid.at[vv, pl.ds((1 - r) * seqs, seqs)], hm.at[1, v], 16, hmsem.at[1], across(u, vv)).start()
+
+        each(hmsend)
+        remote(hid.at[v, pl.ds((1 - r) * seqs, seqs)], hm.at[1, v], 16, hmsem.at[1], partner).start()
+        local(hid.at[v, mine], hm.at[0, v], lsem.at[1]).start()
+        arrived(hm.at[0, 0], lsem.at[1])
     with scope("hand0"):
         hand_over(0)
         hand_over(1)
@@ -501,26 +564,28 @@
         ov = osend.reshape(n, HW, cols)
 
         def down(i, c):
-            at = pl.ds(pl.multiple_of(i * cols, cols), cols)
-            lhs = jnp.concatenate([acto[...], actx[...]], axis=1)
-            ov[i] = dot(lhs, wdn[:, at]).astype(BF)
-
-            def to(d, cc):
-                uu = around(u, d)
-                remote(osend.at[i, uu], gbuf.at[i, u], 19, gsem.at[i], own(uu, v)).start()
-
-            each(to)
-            gbuf[i, u] = osend[i, u]
+            at = pl.ds(pl.multiple_of(i * 2 * cols, 2 * cols), 2 * cols)
+            both = dot(jnp.concatenate([acto[...], actx[...]], axis=1), wdn[:, at]).astype(BF)
+            for h in (0, 1):
+                k = 2 * i + h
+                ov[k] = both[:, h * cols : (h + 1) * cols]
+
+                def to(d, cc):
+                    uu = around(u, d)
+                    remote(osend.at[k, uu], gbuf.at[k, u], 19, gsem.at[k], own(uu, v)).start()
+
+                each(to)
+                gbuf[k, u] = osend[k, u]
             return c
 
-        lax.fori_loop(0, n, down, 0)
+        lax.fori_loop(0, n // 2, down, 0)
 
     with scope("combine"):
         gv = gbuf.reshape(n, HW, cols)
 
         def combine(i, c):
             arrived(gbuf.at[i, most], gsem.at[i])
-            both = dot(ctb[...], gv[i], ((0,), (0,)))
+            both = dot(ctb[...], gv[i])
             csend[i] = (both[:tokens] + both[tokens:]).astype(BF).reshape(n, tok, cols)
 
             def to(d, cc):
@@ -553,12 +618,23 @@
         lax.fori_loop(0, n, final, 0)
 
     with scope("drain"):
-        for send, ref in enumerate((
-            wb.at[most, 0], wb.at[:, 0], res.at[most, 0], res.at[:, 0], wdn.at[last_units], id1.at[most], id2.at[most],
-            xs.at[0, :, pl.ds(0, (2 * n - 1) * seqs)], xs.at[most], rbuf.at[most], hall.at[most], ss1.at[most], hm.at[0, most],
-            town.at[most], ss2.at[most], town, hm.at[1], sso, acts, gbuf.at[most], zbuf.at[:, 0, most], zbuf.at[:, 1],
-        )):
+        sent = {
+            0: wb.at[most, 0], 1: wb.at[most, 0], 4: wdn.at[last_units], 5: id1.at[most], 6: id2.at[most],
+            7: xs.at[0, :, pl.ds(0, (2 * n - 1) * seqs)], 8: xs.at[most], 9: rbuf.at[most], 10: hall.at[most],
+            11: ss1.at[most], 12: hm.at[0, most], 13: town.at[most], 14: ss2.at[most], 15: town, 16: hm.at[1], 17: sso,
+            18: acts, 19: gbuf.at[most], 20: zbuf.at[:, 0, most], 21: zbuf.at[:, 1], 22: res.at[most, 0], 23: res.at[:, 0],
+        }
+        for send, ref in sent.items():
             arrived(ref, ssem.at[send])
+
+        @pl.when(r == 0)
+        def _():
+            arrived(wb.at[0, 0], ssem.at[2])
+            arrived(wb.at[0, 0], ssem.at[3])
+
+        @pl.when(r == 1)
+        def _():
+            arrived(wst, ssem.at[24])
 
 
 def solution(mesh):
@@ -584,7 +660,7 @@
             vmem((seqs, pos, kvw), BF), vmem((seqs, pos, kvw), BF), pltpu.SMEM((seqs,), jnp.int32),
             vmem((model,), BF), vmem((tok, topk), jnp.int32), vmem((tok, topk), F32),
             vmem((model, 2 * hidden), BF), vmem((2 * hidden, half), BF),
-            vmem((n, 2, wrows, cols), BF), vmem((n, 2, seqs, cols), BF),
+            vmem((n, 2, wrows, cols), BF), vmem((n, 2, wrows, cols), BF), vmem((n, 2, seqs, cols), BF),
             vmem((n, n, seqs, HW), BF), vmem((n, n, tokens, HW), BF),
             vmem((n, n, tok, cols), BF), vmem((n, n, tok, cols), BF),
             vmem((n, tok, cols), F32), vmem((tokens, cols), BF), vmem((2, n, seqs, cols), F32),
@@ -597,8 +673,8 @@
             vmem((HW, hidden), BF), vmem((HW, hidden), BF), vmem((HW, hidden), BF),
             vmem((n, n, slots, cols), BF), vmem((n, n, slots, cols), BF),
             vmem((n, n, tok, cols), BF), vmem((n, 2, n, seqs, cols), BF),
-            dma((15,)), dma((22,)), dma((2,)), dma((2,)), dma((n,)), dma((n, n // 2)), dma, dma((2,)), dma((n,)), dma((n,)), dma((n,)),
-            dma, dma, dma, dma, dma((3,)), dma((n,)), dma((n, 2)),
+            dma((15,)), dma((25,)), dma((2, 3)), dma((2,)), dma((n,)), dma((n, n // 2)), dma, dma((2,)), dma((n,)), dma((n,)), dma((n,)),
+            dma, dma, dma, dma, dma((4,)), dma((n,)), dma((n, 2)), pltpu.SemaphoreType.REGULAR((3,)),
         ]
         return pl.pallas_call(
             functools.partial(kernel, n),

time: 91.9 us -> 84.2 us (0.916)
  Pallas kernels: 90.3 us -> 82.7 us
    pallas_call x1, Pallas kernels: 90.3 us -> 82.7 us  [on_device(): pl.pallas_call(functools.partial(kernel, n), out_shape=jax.ShapeDtypeStru...]
where the time goes in v3:
time: 84.2 us; the launch traced here: 84.1 us
  Pallas kernels  82.7 us (98%)
  local copies, waits for them, and re-layouts  1.39 us (2%)
    pallas_call x1, Pallas kernels, on_device(): pl.pallas_call(functools.partial(kernel, n), out_shape=jax.ShapeDtypeStru...  82.7 us

profile of v3, /device:TPU:513, one launch (start us, length us, event | category | flops | bytes accessed | tf_op | source)
XLA Modules:
  0.0 84.1 jit_solution(468875384257026763)
XLA Ops:
  0.0 82.7 %shard_map.136 = bf16[4,4096]{1,0:T(4,128)(2,1)} custom-call(bf16[4,8192]{1,0:T(4,128)(2,1)} %q_hbm.1, bf16[4,512]{1,0:T(4,128)(2,1)} %tk_hbm.1, bf16[4,512]{1,0:T(4,128)(2,1)} %tv_hbm.1, bf16[4,256,512]{2,1,0:T(8,128)(2,1)} %k_hbm.1, bf16[4,256,512]{2,1,0:T(8,128)(2,1)} %v_hbm.1, s32[4]{0:T(128)} %len_hbm.1, bf16[4,4096]{1,0:T(4,128)(2,1)} %res_hbm.1, ...), custom_call_target="tpu_custom_call" | custom-call | tf_op jit(solution)/shard_map/pallas_call | solution.py:679
  82.7 1.4 %copy.16 = bf16[4,4096]{1,0:T(4,128)(2,1)} copy(bf16[4,4096]{1,0:T(4,128)(2,1)} %shard_map.136) | data formatting | bytes 65536

commit v4 on v3

--- a/solution.py
+++ b/solution.py
@@ -86,12 +86,7 @@
     first_units, last_units = pl.ds(0, units), pl.ds(units, units)
     with scope("loads"):
         local(k_hbm, k_s, lsem.at[6]).start()
-
-        def qcopy(h, c):
-            local(q_hbm.at[:, pl.ds(pl.multiple_of(h * HW, HW), HW)], q_s.at[h], lsem.at[0]).start()
-            return c
-
-        lax.fori_loop(0, heads, qcopy, 0)
+        local(q_hbm, q_s, lsem.at[0]).start()
         local(len_hbm, len_s, lsem.at[1]).start()
         local(tk_hbm, tk_s, lsem.at[2]).start()
         local(tv_hbm, tv_s, lsem.at[3]).start()
@@ -99,92 +94,176 @@
         local(ids_hbm, ids_s, lsem.at[4]).start()
         local(rw_hbm, rw_s, lsem.at[5]).start()
 
-    with scope("barrier"):
+    with scope("greet"):
         bar = pltpu.get_barrier_semaphore()
 
-        def peers(sem):
-            def to(d, c):
-                pl.semaphore_signal(sem, device_id={"expert": around(x, d) * n + y, "replica": 1}, device_id_type=mesh_id)
-                pl.semaphore_signal(sem, device_id={"expert": x * n + around(y, d), "replica": 1}, device_id_type=mesh_id)
-                return c
-
-            lax.fori_loop(1, n, to, 0)
-
-        @pl.when(r == 1)
-        def _():
-            peers(bar)
-
-        pl.semaphore_wait(bar, r * 2 * (n - 1) + (1 - r))
-
-        @pl.when(r == 1)
-        def _():
-            pl.semaphore_signal(bar, device_id=partner, device_id_type=mesh_id)
-
-        @pl.when(r == 0)
-        def _():
-            pl.semaphore_signal(ready.at[0], device_id=partner, device_id_type=mesh_id)
-
-    with scope("weights_send"):
-
-        def wsend(d, c):
-            xx, yy = around(x, d), around(y, d)
-            remote(ow_hbm.at[:, columns(0, yy)], wst.at[y, r], 0, wsem.at[0, r], {"expert": x * n + yy, "replica": 1}).start()
-            remote(ow_hbm.at[:, columns(1, xx)], wb.at[x, r], 1, wsem.at[1, r], {"expert": xx * n + y, "replica": 1}).start()
-
-        each(wsend)
-
-        @pl.when(r == 1)
-        def _():
-            local(ow_hbm.at[:, columns(0, y)], wst.at[y, r], lsem.at[9]).start()
-            local(ow_hbm.at[:, columns(1, x)], wb.at[x, r], lsem.at[9]).start()
-
-        @pl.when(r == 0)
-        def _():
-            remote(ow_hbm.at[:, columns(0, y)], wst.at[y, r], 2, wsem.at[0, 2], partner).start()
-            remote(ow_hbm.at[:, columns(1, x)], wb.at[x, r], 3, wsem.at[1, 2], partner).start()
-
-        local(res_hbm.at[:, columns(r, v)], res.at[v, r], lsem.at[10]).start()
-        local(gain_hbm, gain_s, lsem.at[8]).start()
-        local(wg_hbm.at[0], wgu.at[:, first_units], lsem.at[11]).start()
-        local(wu_hbm.at[0], wgu.at[:, last_units], lsem.at[12]).start()
-        local(wd_hbm.at[0, :, pl.ds(pl.multiple_of(r * half, half), half)], wdn.at[first_units], lsem.at[13]).start()
+        def greet(d, c):
+            pl.semaphore_signal(bar, device_id={"expert": around(x, d) * n + y, "replica": r}, device_id_type=mesh_id)
+            pl.semaphore_signal(bar, device_id={"expert": x * n + around(y, d), "replica": r}, device_id_type=mesh_id)
+            return c
+
+        lax.fori_loop(1, n, greet, 0)
 
     with scope("attention"):
         kvh = k_s.shape[2] // HW
         per = heads // kvh
         rows = per * seqs
-        arrived(q_s, lsem.at[0])
+        local(q_hbm, q_s, lsem.at[0]).wait()
         local(len_hbm, len_s, lsem.at[1]).wait()
         local(tk_hbm, tk_s, lsem.at[2]).wait()
         local(tv_hbm, tv_s, lsem.at[3]).wait()
         local(k_hbm, k_s, lsem.at[6]).wait()
         inv_root = 1.0 / math.sqrt(HW)
         rowseq = lax.rem(iota((rows, pos), 0), seqs)
-        colpos = iota((rows, pos), 1)
-        visible = jnp.concatenate(
-            [jnp.where((rowseq == s) & (colpos < len_s[s]), 0.0, NEG) for s in range(seqs)], axis=1
-        )
+        length = functools.reduce(lambda p, t: jnp.where(rowseq == t, len_s[t], p), range(1, seqs), jnp.full((rows, pos), len_s[0]))
+        visible = jnp.where(iota((rows, pos), 1) < length, 0.0, NEG)
         fresh_ok = lax.rem(iota((rows, seqs), 0), seqs) == iota((rows, seqs), 1)
+
+        def of_row(parts):
+            mark = rowseq[:, : parts[0].shape[1]]
+            return functools.reduce(lambda p, t: jnp.where(mark == t, parts[t], p), range(1, seqs), parts[0])
+
         for g in range(kvh):
             at = slice(g * HW, (g + 1) * HW)
-            qg = q_s[g * per : (g + 1) * per].reshape(rows, HW)
+            qg = jnp.concatenate([q_s[:, (g * per + h) * HW : (g * per + h + 1) * HW] for h in range(per)], axis=0)
             kg = k_s[:, :, at].reshape(seqs * pos, HW)
-            s_old = dot(qg, kg, ((1,), (1,))) * inv_root + visible
-            s_new = jnp.where(fresh_ok, dot(qg, tk_s[:, at], ((1,), (1,))) * inv_root, NEG)
-            top = jnp.maximum(jnp.max(s_old, axis=1, keepdims=True), jnp.max(s_new, axis=1, keepdims=True))
+            every = dot(qg, kg, ((1,), (1,)))
+            s_old = of_row([every[:, t * pos : (t + 1) * pos] for t in range(seqs)]) * inv_root + visible
+            s_new = dot(qg, tk_s[:, at], ((1,), (1,))) * inv_root
+            s_new = jnp.max(jnp.where(fresh_ok, s_new, NEG), axis=1, keepdims=True)
+            top = jnp.maximum(jnp.max(s_old, axis=1, keepdims=True), s_new)
             p_old = jnp.exp(s_old - top)
             p_new = jnp.exp(s_new - top)
-            scale = 1.0 / (jnp.sum(p_old, axis=1, keepdims=True) + jnp.sum(p_new, axis=1, keepdims=True))
+            scale = 1.0 / (jnp.sum(p_old, axis=1, keepdims=True) + p_new)
             p_old = (p_old * scale).astype(BF)
             p_new = (p_new * scale).astype(BF).astype(F32)
             if g == 0:
                 local(v_hbm, v_s, lsem.at[7]).wait()
-            vg = v_s[:, :, at].reshape(seqs * pos, HW)
-            mixed = dot(p_old, vg)
+            every = dot(p_old, jnp.concatenate([v_s[t, :, at] for t in range(seqs)], axis=1))
+            mixed = of_row([every[:, t * HW : (t + 1) * HW] for t in range(seqs)])
             tv = tv_s[:, at].astype(F32)
-            for s in range(seqs):
-                mixed = mixed + p_new[:, s : s + 1] * tv[s : s + 1, :]
+            mixed = mixed + p_new * jnp.concatenate([tv] * per, axis=0)
             att[g * (n // kvh) : (g + 1) * (n // kvh)] = mixed.astype(BF).reshape(n // kvh, n, seqs, HW)
+
+    with scope("entry"):
+        pl.semaphore_wait(bar, 2 * (n - 1) + (1 - r))
+
+        @pl.when(r == 1)
+        def _():
+            pl.semaphore_signal(bar, device_id=partner, device_id_type=mesh_id)
+
+        @pl.when(r == 0)
+        def _():
+            pl.semaphore_signal(ready.at[0], device_id=partner, device_id_type=mesh_id)
+
+    def weights_send():
+        def wsend(d, c):
+            xx, yy = around(x, d), around(y, d)
+            remote(ow_hbm.at[:, columns(0, yy)], wst.at[y, r], 0, wsem.at[0, r], {"expert": x * n + yy, "replica": 1}).start()
+            remote(ow_hbm.at[:, columns(1, xx)], wb.at[x, r], 1, wsem.at[1, r], {"expert": xx * n + y, "replica": 1}).start()
+
+        each(wsend)
+
+    mine = pl.ds(r * seqs, seqs)
+
+    def features_send(plane):
+        def t1send(d, c):
+            ahead = d // (n // 2)
+            place = ahead * (2 * (n - d) - 1) + (1 - ahead) * 2 * d
+            rows_at = pl.ds(place * tok + r * seqs, seqs)
+            if plane == 0:
+                xx = around(x, d)
+                remote(att.at[xx], xs.at[y, :, rows_at], 7, t1sem.at[place], {"expert": xx * n + y, "replica": 0}).start()
+            else:
+                yy = around(y, d)
+                remote(att.at[:, yy], xs.at[x, :, rows_at], 7, t1sem.at[place], {"expert": x * n + yy, "replica": 1}).start()
+
+        lax.fori_loop(1, n, lambda i, c: (t1send(far(n - i), c), c)[1], 0)
+
+    with scope("feature_send"):
+
+        @pl.when(r == 0)
+        def _():
+            features_send(0)
+            features_send(1)
+            remote(att.at[:, y], xs.at[x, :, mine], 7, t1sem.at[0], partner).start()
+            weights_send()
+            remote(ow_hbm.at[:, columns(0, y)], wst.at[y, r], 2, wsem.at[0, 2], partner).start()
+            remote(ow_hbm.at[:, columns(1, x)], wb.at[x, r], 3, wsem.at[1, 2], partner).start()
+            local(att.at[x], xs.at[y, :, mine], lsem.at[14]).start()
+
+        @pl.when(r == 1)
+        def _():
+            weights_send()
+            local(ow_hbm.at[:, columns(0, y)], wst.at[y, r], lsem.at[9]).start()
+            local(ow_hbm.at[:, columns(1, x)], wb.at[x, r], lsem.at[9]).start()
+            features_send(1)
+            local(att.at[:, y], xs.at[x, :, mine], lsem.at[14]).start()
+            pl.semaphore_wait(ready.at[0], 1)
+            features_send(0)
+            remote(att.at[x], xs.at[y, :, mine], 7, t1sem.at[0], partner).start()
+
+        local(res_hbm.at[:, columns(r, v)], res.at[v, r], lsem.at[10]).start()
+        local(gain_hbm, gain_s, lsem.at[8]).start()
+        arrived(att.at[0], lsem.at[14])
+
+    chunks = n // 2
+    crows = tokens // chunks
+
+    def chunk_of(w, c):
+        return xs.at[w, :, pl.ds(c * crows, crows)]
+
+    def pass_on(w, c, d):
+        remote(chunk_of(w, c), chunk_of(w, c), 8, xsem.at[w, c], own(u, around(v, d))).start()
+
+    def start_chunk(c):
+        for place in (2 * c, 2 * c + 1):
+            if place == 0:
+                arrived(att.at[0], t1sem.at[0])
+            else:
+                arrived(att.at[pl.ds(0, 2)], t1sem.at[place])
+        for d in (2, n - 2, 1, n - 1):
+            pass_on(v, c, d)
+
+    def relay(c):
+        behind, ahead = around(v, n - 2), around(v, 2)
+        arrived(chunk_of(behind, c), xsem.at[behind, c])
+        if c % 2 == 0:
+            pass_on(behind, c, 2)
+        pass_on(behind, c, 1)
+        arrived(chunk_of(ahead, c), xsem.at[ahead, c])
+        if c % 2 == 1:
+            pass_on(ahead, c, n - 2)
+        pass_on(ahead, c, n - 1)
+
+    def gathered(d):
+        w = around(v, d)
+        for c in range(chunks):
+            arrived(chunk_of(w, c), xsem.at[w, c])
+
+    wv = wb.reshape(n * HW, cols)
+
+    def project(blocks):
+        lhs = jnp.concatenate(
+            [jnp.concatenate([xs[w, k] for k in range(n)], axis=1) for w in blocks], axis=0
+        )
+        part = dot(lhs, wv[...]).astype(BF)
+        for i, w in enumerate(blocks):
+            ysend[:, w] = part[i * tokens : (i + 1) * tokens].reshape(n, tok, cols)
+            rbuf[u, w] = ysend[0, w]
+
+        def to(d, c):
+            uu = around(u, d)
+            ahead = d // (n // 2 + 1)
+            place = (1 - ahead) * (2 * d - 1) + ahead * 2 * (n - d)
+            for w in blocks:
+                remote(ysend.at[place, w], rbuf.at[u, w], 9, rrsem, own(uu, v)).start()
+
+        each(to)
+
+    with scope("gather_start"):
+        start_chunk(0)
+        start_chunk(1)
 
     with scope("ids"):
         local(ids_hbm, ids_s, lsem.at[4]).wait()
@@ -199,56 +278,15 @@
         idt[...] = dot(ids_s[...].astype(F32), place, ((0,), (0,)), exact) + dot(mixing, place_mix, ((0,), (0,)), exact)
         id1[v] = idt[...]
 
-    with scope("barrier_second"):
-
-        @pl.when(r == 1)
-        def _():
-            pl.semaphore_wait(ready.at[0], 1)
-            peers(ready.at[1])
-            pl.semaphore_wait(ready.at[1], 2 * (n - 1))
-            pl.semaphore_signal(ready.at[2], device_id=partner, device_id_type=mesh_id)
-
-        @pl.when(r == 0)
-        def _():
-            pl.semaphore_wait(ready.at[2], 1)
-
-    with scope("feature_send"):
-        mine = pl.ds(r * seqs, seqs)
-
-        @pl.when(r == 0)
-        def _():
-            remote(att.at[:, y], xs.at[x, :, mine], 7, t1sem.at[0], partner).start()
-
-        @pl.when(r == 1)
-        def _():
-            remote(att.at[x], xs.at[y, :, mine], 7, t1sem.at[0], partner).start()
-
-        def t1send(d, c):
-            xx, yy = around(x, d), around(y, d)
-            ahead = d // (n // 2)
-            place = ahead * (2 * (n - d) - 1) + (1 - ahead) * 2 * d
-            rows_at = pl.ds(place * tok + r * seqs, seqs)
-            remote(att.at[xx], xs.at[y, :, rows_at], 7, t1sem.at[place], {"expert": xx * n + y, "replica": 0}).start()
-            remote(att.at[:, yy], xs.at[x, :, rows_at], 7, t1sem.at[place], {"expert": x * n + yy, "replica": 1}).start()
-
-        each(t1send)
-
-        @pl.when(r == 0)
-        def _():
-            local(att.at[x], xs.at[y, :, mine], lsem.at[14]).start()
-
-        @pl.when(r == 1)
-        def _():
-            local(att.at[:, y], xs.at[x, :, mine], lsem.at[14]).start()
-
-        arrived(att.at[0], lsem.at[14])
-
-    with scope("small_send"):
-
         def idsend(d, c):
             remote(idt, id1.at[v], 5, id1sem, own(u, around(v, d))).start()
 
         each(idsend)
+
+    with scope("gather_third"):
+        start_chunk(2)
+
+    with scope("small_send"):
 
         def rsend(d, c):
             vv, uu = around(v, d), around(u, d)
@@ -257,65 +295,13 @@
 
         each(rsend)
         remote(res_hbm.at[:, columns(1 - r, u)], res.at[u, r], 23, rsem.at[1], partner).start()
-        remote(wd_hbm.at[0, :, pl.ds(pl.multiple_of((1 - r) * half, half), half)], wdn.at[last_units], 4, dsem.at[0], partner).start()
-
-    chunks = n // 2
-    crows = tokens // chunks
-
-    def chunk_of(w, c):
-        return xs.at[w, :, pl.ds(c * crows, crows)]
-
-    def pass_on(w, c, d):
-        remote(chunk_of(w, c), chunk_of(w, c), 8, xsem.at[w, c], own(u, around(v, d))).start()
-
-    def start_chunk(c):
-        for place in (2 * c, 2 * c + 1):
-            if place == 0:
-                arrived(att.at[0], t1sem.at[0])
-            else:
-                arrived(att.at[pl.ds(0, 2)], t1sem.at[place])
-        for d in (2, n - 2, 1, n - 1):
-            pass_on(v, c, d)
-
-    def relay(c):
-        behind, ahead = around(v, n - 2), around(v, 2)
-        arrived(chunk_of(behind, c), xsem.at[behind, c])
-        if c % 2 == 0:
-            pass_on(behind, c, 2)
-        pass_on(behind, c, 1)
-        arrived(chunk_of(ahead, c), xsem.at[ahead, c])
-        if c % 2 == 1:
-            pass_on(ahead, c, n - 2)
-        pass_on(ahead, c, n - 1)
-
-    def gathered(d):
-        w = around(v, d)
-        for c in range(chunks):
-            arrived(chunk_of(w, c), xsem.at[w, c])
-
-    wv = wb.reshape(n * HW, cols)
-
-    def project(blocks):
-        lhs = jnp.concatenate(
-            [jnp.concatenate([xs[w, k] for k in range(n)], axis=1) for w in blocks], axis=0
-        )
-        part = dot(lhs, wv[...]).astype(BF)
-        for i, w in enumerate(blocks):
-            ysend[:, w] = part[i * tokens : (i + 1) * tokens].reshape(n, tok, cols)
-            rbuf[u, w] = ysend[0, w]
-
-        def to(d, c):
-            uu = around(u, d)
-            ahead = d // (n // 2 + 1)
-            place = (1 - ahead) * (2 * d - 1) + ahead * 2 * (n - d)
-            for w in blocks:
-                remote(ysend.at[place, w], rbuf.at[u, w], 9, rrsem, own(uu, v)).start()
-
-        each(to)
-
-    with scope("gather_start"):
-        for c in range(chunks):
-            start_chunk(c)
+
+    with scope("gather_last"):
+        start_chunk(3)
+
+    with scope("relay"):
+        for c in range(chunks // 2):
+            relay(c)
     with scope("weights_wait"):
 
         @pl.when(r == 1)
@@ -326,19 +312,15 @@
                 arrived(buf.at[most, 0], wsem.at[p, 1])
                 arrived(buf.at[0, 0], wsem.at[p, 2])
             remote(wst, wb, 24, dsem.at[3], partner).start()
-
-    with scope("ids_second"):
-        arrived(id1.at[most], id1sem)
-        idg[...] = functools.reduce(lambda p, q: p + q, [id1[i] for i in range(n)])
-
-        def id2send(d, c):
-            remote(idg, id2.at[u], 6, id2sem, own(around(u, d), v)).start()
-
-        each(id2send)
-        id2[u] = idg[...]
-    with scope("relay"):
-        for c in range(chunks):
+    with scope("relay_last"):
+        for c in range(chunks // 2, chunks):
             relay(c)
+    with scope("expert_loads"):
+        local(wg_hbm.at[0], wgu.at[:, first_units], lsem.at[11]).start()
+        local(wu_hbm.at[0], wgu.at[:, last_units], lsem.at[12]).start()
+        local(wd_hbm.at[0, :, pl.ds(pl.multiple_of(r * half, half), half)], wdn.at[first_units], lsem.at[13]).start()
+        remote(wd_hbm.at[0, :, pl.ds(pl.multiple_of((1 - r) * half, half), half)], wdn.at[last_units], 4, dsem.at[0], partner).start()
+
     with scope("weights_wait2"):
 
         @pl.when(r == 0)
@@ -354,15 +336,22 @@
         project([around(v, 1), around(v, n - 1)])
     with scope("project2"):
         project([around(v, 2), around(v, n - 2)])
+    with scope("ids_second"):
+        arrived(id1.at[most], id1sem)
+        idg[...] = functools.reduce(lambda p, q: p + q, [id1[i] for i in range(n)])
+
+        def id2send(d, c):
+            remote(idg, id2.at[u], 6, id2sem, own(around(u, d), v)).start()
+
+        each(id2send)
+        id2[u] = idg[...]
     with scope("gather3"):
         gathered(3)
         gathered(n - 3)
-    with scope("project3"):
-        project([around(v, 3), around(v, n - 3)])
     with scope("gather4"):
         gathered(n // 2)
-    with scope("project4"):
-        project([around(v, n // 2)])
+    with scope("project3"):
+        project([around(v, 3), around(v, n - 3), around(v, n // 2)])
 
     with scope("tables_wait"):
         arrived(id2.at[most], id2sem)
@@ -489,17 +478,6 @@
         ss2[u] = ss2t[...]
     with scope("pack4"):
         pack_pair(4)
-    with scope("hidden_home"):
-
-        def hmsend(d, c):
-            vv = around(v, d)
-            remote(hid.at[vv, mine], hm.at[0, v], 12, hmsem.at[0], own(u, vv)).start()
-            remote(hid.at[vv, pl.ds((1 - r) * seqs, seqs)], hm.at[1, v], 16, hmsem.at[1], across(u, vv)).start()
-
-        each(hmsend)
-        remote(hid.at[v, pl.ds((1 - r) * seqs, seqs)], hm.at[1, v], 16, hmsem.at[1], partner).start()
-        local(hid.at[v, mine], hm.at[0, v], lsem.at[1]).start()
-        arrived(hm.at[0, 0], lsem.at[1])
     with scope("hand0"):
         hand_over(0)
         hand_over(1)
@@ -555,6 +533,17 @@
         for t in range(up_at):
             acts[:, t * HW : (t + 1) * HW] = swapped(scr.at[t]).astype(BF)
         remote(acts, actx, 18, dsem.at[2], partner).start()
+    with scope("hidden_home"):
+
+        def hmsend(d, c):
+            vv = around(v, d)
+            remote(hid.at[vv, mine], hm.at[0, v], 12, hmsem.at[0], own(u, vv)).start()
+            remote(hid.at[vv, pl.ds((1 - r) * seqs, seqs)], hm.at[1, v], 16, hmsem.at[1], across(u, vv)).start()
+
+        each(hmsend)
+        remote(hid.at[v, pl.ds((1 - r) * seqs, seqs)], hm.at[1, v], 16, hmsem.at[1], partner).start()
+        local(hid.at[v, mine], hm.at[0, v], lsem.at[1]).start()
+        arrived(hm.at[0, 0], lsem.at[1])
     with scope("activation_wait"):
         local(wd_hbm.at[0, :, pl.ds(0, half)], wdn.at[first_units], lsem.at[13]).wait()
         arrived(wdn.at[last_units], dsem.at[0])
@@ -563,22 +552,24 @@
     with scope("down"):
         ov = osend.reshape(n, HW, cols)
 
-        def down(i, c):
-            at = pl.ds(pl.multiple_of(i * 2 * cols, 2 * cols), 2 * cols)
-            both = dot(jnp.concatenate([acto[...], actx[...]], axis=1), wdn[:, at]).astype(BF)
-            for h in (0, 1):
-                k = 2 * i + h
-                ov[k] = both[:, h * cols : (h + 1) * cols]
-
-                def to(d, cc):
+        def down(first, count):
+            at = slice(first * cols, (first + count) * cols)
+            part = dot(jnp.concatenate([acto[...], actx[...]], axis=1), wdn[:, at]).astype(BF)
+            for h in range(count):
+                k = first + h
+                ov[k] = part[:, h * cols : (h + 1) * cols]
+
+                def to(d, c):
                     uu = around(u, d)
                     remote(osend.at[k, uu], gbuf.at[k, u], 19, gsem.at[k], own(uu, v)).start()
 
                 each(to)
                 gbuf[k, u] = osend[k, u]
-            return c
-
-        lax.fori_loop(0, n // 2, down, 0)
+
+        down(0, 1)
+        down(1, 1)
+        for first in range(2, n, 2):
+            down(first, 2)
 
     with scope("combine"):
         gv = gbuf.reshape(n, HW, cols)
@@ -656,7 +647,7 @@
         vmem = pltpu.VMEM
         dma = pltpu.SemaphoreType.DMA
         scratch = [
-            vmem((heads, seqs, HW), BF), vmem((seqs, kvw), BF), vmem((seqs, kvw), BF),
+            vmem((seqs, heads * HW), BF), vmem((seqs, kvw), BF), vmem((seqs, kvw), BF),
             vmem((seqs, pos, kvw), BF), vmem((seqs, pos, kvw), BF), pltpu.SMEM((seqs,), jnp.int32),
             vmem((model,), BF), vmem((tok, topk), jnp.int32), vmem((tok, topk), F32),
             vmem((model, 2 * hidden), BF), vmem((2 * hidden, half), BF),
@@ -674,11 +665,11 @@
             vmem((n, n, slots, cols), BF), vmem((n, n, slots, cols), BF),
             vmem((n, n, tok, cols), BF), vmem((n, 2, n, seqs, cols), BF),
             dma((15,)), dma((25,)), dma((2, 3)), dma((2,)), dma((n,)), dma((n, n // 2)), dma, dma((2,)), dma((n,)), dma((n,)), dma((n,)),
-            dma, dma, dma, dma, dma((4,)), dma((n,)), dma((n, 2)), pltpu.SemaphoreType.REGULAR((3,)),
+            dma, dma, dma, dma, dma((4,)), dma((n,)), dma((n, 2)), pltpu.SemaphoreType.REGULAR((1,)),
         ]
         return pl.pallas_call(
             functools.partial(kernel, n),
-            out_shape=jax.ShapeDtypeStruct(residual.shape, BF),
+            out_shape=pltpu.VMEM(residual.shape, BF),
             in_specs=[pl.BlockSpec(memory_space=pl.ANY)] * 14,
             out_specs=pl.BlockSpec(memory_space=pltpu.VMEM),
             scratch_shapes=scratch,

time: 84.2 us -> 81 us (0.962)
  Pallas kernels: 82.7 us -> 80.2 us
    pallas_call x1, Pallas kernels: 82.7 us -> 80.2 us  [on_device(): pl.pallas_call(functools.partial(kernel, n), out_shape=pltpu.VMEM(residua...]
where the time goes in v4:
time: 81 us; the launch traced here: 80.8 us
  Pallas kernels  80.2 us (99%)
    pallas_call x1, Pallas kernels, on_device(): pl.pallas_call(functools.partial(kernel, n), out_shape=pltpu.VMEM(residua...  80.2 us

profile of v4, /device:TPU:513, one launch (start us, length us, event | category | flops | bytes accessed | tf_op | source)
XLA Modules:
  0.0 80.8 jit_solution(5314352603468624604)
XLA Ops:
  0.0 80.2 %shard_map.136 = bf16[4,4096]{1,0:T(4,128)(2,1)S(1)} custom-call(bf16[4,8192]{1,0:T(4,128)(2,1)} %q_hbm.1, bf16[4,512]{1,0:T(4,128)(2,1)} %tk_hbm.1, bf16[4,512]{1,0:T(4,128)(2,1)} %tv_hbm.1, bf16[4,256,512]{2,1,0:T(8,128)(2,1)} %k_hbm.1, bf16[4,256,512]{2,1,0:T(8,128)(2,1)} %v_hbm.1, s32[4]{0:T(128)} %len_hbm.1, bf16[4,4096]{1,0:T(4,128)(2,1)} %res_hbm.1, ...), custom_call_target="tpu_custom_call" | custom-call | tf_op jit(solution)/shard_map/pallas_call | solution.py:670
  80.2 0.6 copy.16
